TPU v7x, 256 devices: a whole 4x4x8 slice. The times are simulated.
256 devices in a mesh: row: 16 (over y, z_lo), col: 16 (over z_hi, x, core).
Axes of the slice: x: 4, y: 4, z: 8 (z_hi: 2, z_lo: 4; z = z_hi * 4 + z_lo), core: 2. Of those that a mesh axis runs over, the one named last changes fastest.
Arguments:
- archive: float32 [65536, 256], P('row'), may hold values from -6 to 6
- slab_index: int32 [12288], replicated, may hold values from 0 to 65535
- targets: float32 [12288, 256], P('col'), may hold values from -6 to 6
Outputs:
- panels: float32 [12288, 512], P('row')
- applied: float32 [12288, 256], P(('row', 'col'))
Inputs may be any that keep to these rules, and one draw needn't show every extreme that they name: `slab_index`: values may repeat.
All inputs are finite; a program needn't handle non-finite values.
Results may differ from a plain program's by a relative error of at most 0.0003.
Values sent between devices are 32-bit elements; how exact they have to be, the bound alone decides.
No kernel may reach another device: no remote copies, remote signals or barrier semaphores. Data moves between devices by JAX's collectives and lax.ppermute only.
A program may use at most 64 MiB of HBM per device.

v0:
```python
import functools

import jax
import jax.numpy as jnp
from jax import lax
from jax.experimental import pallas as pl
from jax.experimental.pallas import tpu as pltpu
from jax.sharding import PartitionSpec as P


ORDER = 12288
F = 256
NB = 256
PANELS = 2
NT = 256
LEAD = PANELS * NB
SIDE = 16
LOCAL = ORDER // SIDE
PIECE = LOCAL // SIDE
LEAD_PIECE = LEAD // 8
TILES = LOCAL // NB
HALF = LOCAL // 2
ROUND = 8

precise = lax.Precision.HIGHEST
nugget = 1.0
scale = 5.0**0.5 / 16.0


def row_swap(value, dy, dz):
    pairs = [(y * 4 + z, (y ^ dy) * 4 + (z ^ dz)) for y in range(4) for z in range(4)]
    return lax.ppermute(value, "row", pairs)


def col_swap(value, dh, dx, dk):
    pairs = [
        ((h * 4 + x) * 2 + k, ((h ^ dh) * 4 + (x ^ dx)) * 2 + (k ^ dk))
        for h in range(2)
        for x in range(4)
        for k in range(2)
    ]
    return lax.ppermute(value, "col", pairs)


def flip(value):
    pairs = [(r * SIDE + c, c * SIDE + r) for r in range(SIDE) for c in range(SIDE)]
    return lax.ppermute(value, ("row", "col"), pairs)


def dot(left, right, left_dim, right_dim, precision=None):
    return lax.dot_general(
        left,
        right,
        (((left_dim,), (right_dim,)), ((), ())),
        precision=precision,
        preferred_element_type=jnp.float32,
    )


def split(value):
    high = value.astype(jnp.bfloat16)
    low = (value - high.astype(jnp.float32)).astype(jnp.bfloat16)
    return high, low


def dot3(left, right, left_dim, right_dim):
    left_high, left_low = left
    right_high, right_low = right
    small = dot(left_high, right_low, left_dim, right_dim) + dot(left_low, right_high, left_dim, right_dim)
    return small + dot(left_high, right_high, left_dim, right_dim)


def lane_squares(value):
    square = value * value
    ones = jnp.ones((8, square.shape[1]), jnp.float32)
    return dot(ones, square, 1, 1, precise)[0:1, :]


def matern(left_sq, right_sq, cross):
    clipped = jnp.maximum(left_sq + right_sq + cross, scale * scale)
    scaled = clipped * lax.rsqrt(clipped)
    return (1.0 + scaled + clipped * (1.0 / 3.0)) * jnp.exp(-scaled)


def eliminate(rows):
    lane = lax.broadcasted_iota(jnp.int32, (8, 128), 1)
    sub = lax.broadcasted_iota(jnp.int32, (8, 128), 0)
    pivots = [None] * 16

    def across(value, index):
        return jnp.broadcast_to(value[:, index : index + 1], (8, 128))

    def down(value, index):
        return jnp.broadcast_to(value[index : index + 1, :], (8, 128))

    for start in range(0, 128, ROUND):
        first = start // 8
        columns = [{v: across(rows[v], start + t) for v in range(first, 16)} for t in range(ROUND)]
        for t in range(ROUND):
            own, inner = (start + t) // 8, (start + t) % 8
            pivot = down(columns[t][own], inner)
            inverse = 1.0 / pivot
            pivots[own] = pivot if inner == 0 else jnp.where(sub >= inner, pivot, pivots[own])
            row = jnp.where(lane == start + t, 1.0 + pivot, down(rows[own], inner))
            later = [down(columns[u][own], inner) for u in range(t + 1, ROUND)]
            for v in range(own, 16):
                if v == own and inner == 7:
                    continue
                factor = columns[t][v] * inverse
                if v == own:
                    factor = jnp.where(sub > inner, factor, 0.0)
                rows[v] = rows[v] - factor * row
                for u in range(t + 1, ROUND):
                    columns[u][v] = columns[u][v] - factor * later[u - t - 1]
    result = []
    for v in range(16):
        unit = jnp.where(lane < sub + 8 * v, rows[v], jnp.where(lane == sub + 8 * v, 1.0, 0.0))
        result.append(unit * lax.rsqrt(pivots[v]))
    return jnp.concatenate(result, axis=0)


def aligned(start):
    return pl.multiple_of(start, 8)


def aligned(start):
    return pl.multiple_of(start, 8)


def whole(pair):
    return pair[0][...], pair[1][...]


def gram_kernel(place_ref, own_ref, other_ref, lead_ref, out_ref):
    x, k = place_ref[3], place_ref[4]
    for s in range(4):
        at = (x ^ s) * 2
        lead_ref[pl.ds(aligned((at + k) * LEAD_PIECE), LEAD_PIECE), :] = own_ref[s] * scale
        lead_ref[pl.ds(aligned((at + 1 - k) * LEAD_PIECE), LEAD_PIECE), :] = other_ref[s] * scale
    lead = lead_ref[...]
    left_sq = jnp.sum(lead * lead, axis=1, keepdims=True)
    block = matern(left_sq, lane_squares(lead), dot(lead, lead * -2.0, 1, 1, precise))
    row = lax.broadcasted_iota(jnp.int32, (LEAD, LEAD), 0)
    lane = lax.broadcasted_iota(jnp.int32, (LEAD, LEAD), 1)
    out_ref[...] = block + jnp.where(row == lane, nugget, 0.0)


def factor_kernel(first, in_ref, out_ref):
    out_ref[...] = in_ref[...]
    tall = lax.broadcasted_iota(jnp.int32, (LEAD - first, 128), 0) + first
    wide = lax.broadcasted_iota(jnp.int32, (128, LEAD), 1)

    def step(index, carry):
        off = pl.multiple_of(index * 128, 128)
        here = pl.ds(off, 128)
        inverse = eliminate([out_ref[pl.ds(off + 8 * v, 8), here] for v in range(16)])
        later = tall >= off + 128
        below = jnp.where(later, dot(out_ref[first:, here], inverse, 1, 1, precise), 0.0)
        across = dot(inverse, out_ref[here, :], 1, 0, precise)
        out_ref[first:, here] = jnp.where(later, 0.0, out_ref[first:, here])
        out_ref[here, :] = across
        out_ref[here, here] = inverse
        across = out_ref[here, :]
        out_ref[first:, :] = out_ref[first:, :] - dot(below, across, 1, 0, precise)
        out_ref[here, :] = jnp.where(wide < off + 128, across, 0.0)
        return carry

    lax.fori_loop(first // 128, first // 128 + 2, step, 0)


def slab_kernel(
    place_ref, own_rows, other_rows, c0, c1, c2, c3, lead_ref, inverse_ref, targets_ref,
    panel_ref, part_other_ref, part_own_ref,
    left_ref, sum_ref, cols_ref, cols_high, cols_low, goal_high, goal_low, lead_high, lead_low, inv_high, inv_low,
):
    y, z, h, x, k, row_place, col_place = (place_ref[i] for i in range(7))
    for a, ref in enumerate((c0, c1, c2, c3)):
        for b in range(4):
            at = (y ^ a) * 4 + (z ^ b)
            cols_ref[pl.ds(aligned(at * PIECE), PIECE), :] = ref[b] * scale
    left_ref[:HALF] = other_rows[...].reshape(HALF, F) * scale
    left_ref[HALF:] = own_rows[...].reshape(HALF, F) * scale
    cols_high[...], cols_low[...] = split(cols_ref[...] * -2.0)
    goal_high[...], goal_low[...] = split(targets_ref[...])
    lead_high[...], lead_low[...] = split(lead_ref[...] * -2.0)
    inv_high[...], inv_low[...] = split(inverse_ref[...])
    cols, goal, inv, lead = (cols_high, cols_low), (goal_high, goal_low), (inv_high, inv_low), (lead_high, lead_low)
    lead_lane = lane_squares(lead_ref[...])
    col_lane = lane_squares(cols_ref[...])

    left = lead_ref[...]
    block = matern(jnp.sum(left * left, axis=1, keepdims=True), col_lane, dot3(split(left), whole(cols), 1, 1))
    gram = dot3(split(block), whole(goal), 1, 0)
    nuggets = [targets_ref[:NB, :] * jnp.where(col_place == p, nugget, 0.0) for p in range(PANELS)]
    gram = gram + jnp.concatenate(nuggets, axis=0)
    weights = split(dot3(whole(inv), split(gram), 1, 0))
    same = jnp.where(row_place == col_place, nugget, 0.0)

    def panel_step(side, carry):
        core = jnp.where(side == 0, 1 - k, k)
        where = pl.ds(aligned(side * HALF), HALF)
        starts = [
            aligned((((h ^ e) * 4 + (x ^ s)) * 2 + core) * PIECE) for s in range(4) for e in range(2)
        ]
        left = left_ref[where, :]
        left_sq = jnp.sum(left * left, axis=1, keepdims=True)
        pair = split(left)
        block = matern(left_sq, lead_lane, dot3(pair, whole(lead), 1, 1))
        row = jnp.concatenate([lax.broadcasted_iota(jnp.int32, (PIECE, 1), 0) + start for start in starts], axis=0)
        spot = jnp.where(row < NB, row + row_place * NB, LEAD)
        lane = lax.broadcasted_iota(jnp.int32, (HALF, LEAD), 1)
        block = block + jnp.where(spot == lane, nugget, 0.0)
        panel = dot3(split(block), whole(inv), 1, 1)
        for n, start in enumerate(starts):
            panel_ref[pl.ds(start, PIECE), :] = panel[n * PIECE : n * PIECE + PIECE]
        block = matern(left_sq, col_lane, dot3(pair, whole(cols), 1, 1))
        diag = jnp.concatenate([targets_ref[pl.ds(start, PIECE), :] for start in starts], axis=0)
        sum_ref[where, :] = dot3(split(block), whole(goal), 1, 0) + diag * same - dot3(split(panel), weights, 1, 0)
        return carry

    lax.fori_loop(0, 2, panel_step, 0)
    part_other_ref[...] = sum_ref[:HALF, :].reshape(4, 2, PIECE, NT)
    part_own_ref[...] = sum_ref[HALF:, :].reshape(4, 2, PIECE, NT)


def per_device(archive, slab_index, targets):
    row_place = lax.axis_index("row")
    col_place = lax.axis_index("col")
    y, z = row_place // 4, row_place % 4
    h, x, k = col_place // 8, col_place // 2 % 4, col_place % 2
    shard = archive.shape[0]
    smem = pl.BlockSpec(memory_space=pltpu.SMEM)
    vmem = pl.BlockSpec(memory_space=pltpu.VMEM)
    f32, bf16 = jnp.float32, jnp.bfloat16

    def array(kind, *shape):
        return jax.ShapeDtypeStruct(shape, kind)

    def near(array):
        return pltpu.with_memory_space_constraint(array, pltpu.VMEM)

    def call(kernel, name, outs, scratch, place, *args):
        return pl.pallas_call(
            kernel,
            out_shape=tuple(s if far else pltpu.VMEM(s.shape, s.dtype) for s, far in outs),
            in_specs=([] if place is None else [smem]) + [vmem] * len(args),
            out_specs=tuple(vmem for _ in outs),
            scratch_shapes=[pltpu.VMEM(s.shape, s.dtype) for s in scratch],
            compiler_params=pltpu.CompilerParams(vmem_limit_bytes=(40 if name == "slab" else 16) << 20),
        )(*([] if place is None else [place]), *args)

    def three(shift):
        received = []
        for s in (1, 2, 3):
            received.append(shift(s))
        return received

    place = jnp.stack([y, z, h, x, k, row_place, col_place]).astype(jnp.int32)

    stored = slab_index.reshape(TILES, SIDE, NB).transpose(1, 0, 2).reshape(SIDE, LOCAL)
    wanted = lax.dynamic_slice_in_dim(stored, col_place * PIECE, PIECE, 1).reshape(2, 2, 2, 2, PIECE)
    for axis, bit in enumerate((y // 2, y % 2, z // 2, z % 2)):
        wanted = jnp.where(bit == 1, jnp.flip(wanted, axis), wanted)
    lead_ids = lax.dynamic_slice_in_dim(stored[:PANELS, :NB].reshape(-1), (x * 2 + k) * LEAD_PIECE, LEAD_PIECE, 0)
    ids = jnp.concatenate([lead_ids, wanted.reshape(-1)]) - row_place * shard
    inside = (ids >= 0) & (ids < shard)
    picked = jnp.take(archive, jnp.clip(ids, 0, shard - 1), axis=0)
    picked = jnp.where(inside[:, None], picked, 0.0)

    early = picked[:LEAD_PIECE]
    lead = early + sum(three(lambda s: row_swap(early, s, 0)))
    lead_sum = lead
    lead = lead + sum(three(lambda s: row_swap(lead_sum, 0, s)))
    lead_own = jnp.stack([lead] + three(lambda s: col_swap(lead, 0, s, 0)))
    lead_other = col_swap(lead_own, 0, 0, 1)

    picked = picked[LEAD_PIECE:].reshape(4, 4, PIECE, F)
    mine = picked[0] + sum(three(lambda s: row_swap(picked[s], s, 0)))
    piece = mine[0] + sum(three(lambda s: row_swap(mine[s], 0, s)))

    pair = jnp.stack([piece, col_swap(piece, 1, 0, 0)])
    rows_own = jnp.stack([pair] + three(lambda s: col_swap(pair, 0, s, 0)))
    rows_other = col_swap(rows_own, 0, 0, 1)
    turned = flip(piece)
    quarter = jnp.stack([turned] + three(lambda s: row_swap(turned, 0, s)))
    cols = [quarter] + three(lambda s: row_swap(quarter, s, 0))

    square = (array(f32, LEAD, LEAD), False)
    lead_all, inverse = call(
        gram_kernel, "gram", ((array(f32, LEAD, F), False), square), (), place, near(lead_own), near(lead_other)
    )
    for first in (0, LEAD // 2):
        (inverse,) = call(
            functools.partial(factor_kernel, first), f"factor{first}", (square,), (), None, near(inverse)
        )
    panels, part_other, part_own = call(
        slab_kernel,
        "slab",
        (
            (array(f32, LOCAL, LEAD), True),
            (array(f32, 4, 2, PIECE, NT), False),
            (array(f32, 4, 2, PIECE, NT), False),
        ),
        (array(f32, LOCAL, F), array(f32, LOCAL, NT), array(f32, LOCAL, F))
        + (array(bf16, LOCAL, F),) * 4
        + (array(bf16, LEAD, F),) * 2
        + (array(bf16, LEAD, LEAD),) * 2,
        place, near(rows_own), near(rows_other), *(near(c) for c in cols), near(lead_all), near(inverse), targets,
    )

    total = part_own + col_swap(part_other, 0, 0, 1)
    result = total[0] + sum(three(lambda s: col_swap(total[s], 0, s, 0)))
    result = result[0] + col_swap(result[1], 1, 0, 0)
    return (panels, result)


def solution(mesh):
    placed = (P("row", None), P(), P("col", None))
    return jax.shard_map(
        per_device,
        mesh=mesh,
        in_specs=placed,
        out_specs=(P("row", None), P(("row", "col"), None)),
        check_vma=False,
    )
```

profile of v0, /device:TPU:1, one launch (start us, length us, event | category | flops | bytes accessed | tf_op | source)
XLA Modules:
  0.0 124.0 jit_solution(12940612169581553019)
XLA Ops:
  0.7 0.8 reshape.92
  1.6 0.1 dynamic-slice_bitcast_fusion
  1.7 0.1 dynamic_slice.6
  1.7 0.1 constant_dynamic-slice_fusion
  1.9 0.1 concatenate.26
  2.0 0.1 concatenate.23
  2.1 0.1 fusion.3
  2.2 0.1 compare_and_fusion.1
  2.3 4.9 %gather_fusion = f32[832,256]{1,0:T(8,128)S(1)} fusion(f32[4096,256]{1,0:T(8,128)} %param.3, s32[1024]{0:T(1024)S(1)} %pad_clamp_fusion), kind=kCustom, calls=%fused_computation | custom fusion | bytes 1707264 | tf_op jit(solution)/shard_map/jit(_take)/gather | solution.py:267
  7.1 0.3 select_select_fusion
  7.4 0.1 fusion.6
  7.5 3.6 %collective-permute-start.2 = (f32[4,48,256]{2,1,0:T(8,128)S(1)}, f32[4,48,256]{2,1,0:T(8,128)S(1)}, u32[]{:S(2)}, u32[]{:S(2)}) collective-permute-start(f32[4,48,256]{2,1,0:T(8,128)S(1)} %bitcast.65), channel_id=1, source_target_pairs={{0,192},{16,208},{32,224},{48,240},{64,128},{80,144},{96,160},{112... | collective-permute-start | bytes 589832 | tf_op jit(solution)/shard_map/ppermute | solution.py:32
  11.1 0.3 collective-permute-start.1
  11.5 0.3 collective-permute-start
  11.8 7.6 %collective-permute-done.2 = f32[4,48,256]{2,1,0:T(8,128)S(1)} collective-permute-done((f32[4,48,256]{2,1,0:T(8,128)S(1)}, f32[4,48,256]{2,1,0:T(8,128)S(1)}, u32[]{:S(2)}, u32[]{:S(2)}) %collective-permute-start.2) | collective-permute-done | bytes 196640 | tf_op jit(solution)/shard_map/ppermute | solution.py:32
  19.4 0.0 collective-permute-done.1
  19.4 0.0 collective-permute-done
  19.4 0.1 add_add_fusion
  19.5 0.0 copy-start
  19.5 3.9 %collective-permute-start.4 = (f32[48,256]{1,0:T(8,128)S(1)}, f32[48,256]{1,0:T(8,128)S(1)}, u32[]{:S(2)}, u32[]{:S(2)}) collective-permute-start(f32[48,256]{1,0:T(8,128)S(1)} %get-tuple-element.19), channel_id=1, source_target_pairs={{0,32},{16,48},{32,0},{48,16},{64,96},{80,112},{96,64},{112,80},{1... | collective-permute-start | bytes 147464 | tf_op jit(solution)/shard_map/ppermute | solution.py:32
  23.5 1.5 %collective-permute-start.5 = (f32[48,256]{1,0:T(8,128)S(1)}, f32[48,256]{1,0:T(8,128)S(1)}, u32[]{:S(2)}, u32[]{:S(2)}) collective-permute-start(f32[48,256]{1,0:T(8,128)S(1)} %get-tuple-element.20), channel_id=1, source_target_pairs={{0,48},{16,32},{32,16},{48,0},{64,112},{80,96},{96,80},{112,64},{1... | collective-permute-start | bytes 147464 | tf_op jit(solution)/shard_map/ppermute | solution.py:32
  24.9 0.2 collective-permute-start.3
  25.1 2.7 %collective-permute-start.20 = (f32[64,256]{1,0:T(8,128)S(1)}, f32[64,256]{1,0:T(8,128)S(1)}, u32[]{:S(2)}, u32[]{:S(2)}) collective-permute-start(f32[64,256]{1,0:T(8,128)S(1)} %slice.84), channel_id=1, source_target_pairs={{0,192},{16,208},{32,224},{48,240},{64,128},{80,144},{96,160},{112... | collective-permute-start | bytes 196616 | tf_op jit(solution)/shard_map/ppermute | solution.py:32
  27.8 0.1 collective-permute-start.19
  27.9 0.0 collective-permute-done.4
  27.9 0.6 collective-permute-start.18
  28.5 0.2 collective-permute-done.5
  28.8 5.6 %collective-permute-start.6 = (f32[48,256]{1,0:T(8,128)S(1)}, f32[48,256]{1,0:T(8,128)S(1)}, u32[]{:S(2)}, u32[]{:S(2)}) collective-permute-start(f32[48,256]{1,0:T(8,128)S(1)} %fusion.2), channel_id=1, source_target_pairs={{0,8},{1,9},{2,10},{3,11},{4,12},{5,13},{6,14},{7,15},{8,0},{9,1},... | collective-permute-start | bytes 147464 | tf_op jit(solution)/shard_map/ppermute | solution.py:42
  34.4 0.0 collective-permute-done.20
  34.4 0.0 collective-permute-done.19
  34.4 0.0 collective-permute-done.18
  34.4 1.7 %collective-permute-start.23 = (f32[64,256]{1,0:T(8,128)S(1)}, f32[64,256]{1,0:T(8,128)S(1)}, u32[]{:S(2)}, u32[]{:S(2)}) collective-permute-start(f32[64,256]{1,0:T(8,128)S(1)} %add_add_fusion.2), channel_id=1, source_target_pairs={{0,48},{16,32},{32,16},{48,0},{64,112},{80,96},{96,80},{112,64},{1... | collective-permute-start | bytes 196616 | tf_op jit(solution)/shard_map/ppermute | solution.py:32
  36.1 0.3 collective-permute-start.22
  36.5 1.6 %collective-permute-start.21 = (f32[64,256]{1,0:T(8,128)S(1)}, f32[64,256]{1,0:T(8,128)S(1)}, u32[]{:S(2)}, u32[]{:S(2)}) collective-permute-start(f32[64,256]{1,0:T(8,128)S(1)} %add_add_fusion.2), channel_id=1, source_target_pairs={{0,16},{16,0},{32,48},{48,32},{64,80},{80,64},{96,112},{112,96},{1... | collective-permute-start | bytes 196616 | tf_op jit(solution)/shard_map/ppermute | solution.py:32
  38.1 6.0 %collective-permute-start.11 = (f32[48,256]{1,0:T(8,128)S(1)}, f32[48,256]{1,0:T(8,128)S(1)}, u32[]{:S(2)}, u32[]{:S(2)}) collective-permute-start(f32[48,256]{1,0:T(8,128)S(1)} %fusion.2), channel_id=1, source_target_pairs={{0,0},{1,16},{2,32},{3,48},{4,64},{5,80},{6,96},{7,112},{8,128},{9... | collective-permute-start | bytes 147464 | tf_op jit(solution)/shard_map/ppermute | solution.py:47
  44.1 3.6 %collective-permute-start.8 = (f32[2,48,256]{2,1,0:T(8,128)S(1)}, f32[2,48,256]{2,1,0:T(8,128)S(1)}, u32[]{:S(2)}, u32[]{:S(2)}) collective-permute-start(f32[2,48,256]{2,1,0:T(8,128)S(1)} %get-tuple-element.23), channel_id=1, source_target_pairs={{0,4},{1,5},{2,6},{3,7},{4,0},{5,1},{6,2},{7,3},{8,12},{9,13},{10,... | collective-permute-start | bytes 294920 | tf_op jit(solution)/shard_map/ppermute | solution.py:42
  47.7 1.5 %collective-permute-start.7 = (f32[2,48,256]{2,1,0:T(8,128)S(1)}, f32[2,48,256]{2,1,0:T(8,128)S(1)}, u32[]{:S(2)}, u32[]{:S(2)}) collective-permute-start(f32[2,48,256]{2,1,0:T(8,128)S(1)} %get-tuple-element.23), channel_id=1, source_target_pairs={{0,2},{1,3},{2,0},{3,1},{4,6},{5,7},{6,4},{7,5},{8,10},{9,11},{10,... | collective-permute-start | bytes 294920 | tf_op jit(solution)/shard_map/ppermute | solution.py:42
  49.3 2.8 %collective-permute-start.26 = (f32[64,256]{1,0:T(8,128)S(1)}, f32[64,256]{1,0:T(8,128)S(1)}, u32[]{:S(2)}, u32[]{:S(2)}) collective-permute-start(f32[64,256]{1,0:T(8,128)S(1)} %add_add_fusion.1), channel_id=1, source_target_pairs={{0,6},{1,7},{2,4},{3,5},{4,2},{5,3},{6,0},{7,1},{8,14},{9,15},{10,... | collective-permute-start | bytes 196616 | tf_op jit(solution)/shard_map/ppermute | solution.py:42
  52.0 1.0 collective-permute-start.24
  53.0 1.6 %collective-permute-done.7 = f32[2,48,256]{2,1,0:T(8,128)S(1)} collective-permute-done((f32[2,48,256]{2,1,0:T(8,128)S(1)}, f32[2,48,256]{2,1,0:T(8,128)S(1)}, u32[]{:S(2)}, u32[]{:S(2)}) %collective-permute-start.7) | collective-permute-done | bytes 98336 | tf_op jit(solution)/shard_map/ppermute | solution.py:42
  54.7 0.0 collective-permute-start.14
  54.7 2.0 %collective-permute-start.13 = (f32[48,256]{1,0:T(8,128)S(1)}, f32[48,256]{1,0:T(8,128)S(1)}, u32[]{:S(2)}, u32[]{:S(2)}) collective-permute-start(f32[48,256]{1,0:T(8,128)S(1)} %collective-permute-done.11), channel_id=1, source_target_pairs={{0,32},{16,48},{32,0},{48,16},{64,96},{80,112},{96,64},{112,80},{1... | collective-permute-start | bytes 147464 | tf_op jit(solution)/shard_map/ppermute | solution.py:32
  56.7 0.6 collective-permute-done.26
  57.3 1.1 collective-permute-start.12
  58.3 2.3 %collective-permute-start.10 = (f32[4,2,48,256]{3,2,1,0:T(8,128)S(1)}, f32[4,2,48,256]{3,2,1,0:T(8,128)S(1)}, u32[]{:S(2)}, u32[]{:S(2)}) collective-permute-start(f32[4,2,48,256]{3,2,1,0:T(8,128)S(1)} %pad_maximum_fusion.own_rows), channel_id=1, source_target_pairs={{0,1},{1,0},{2,3},{3,2},{4,5},{5,4},{6,7},{7,6},{8,9},{9,8},{10,11... | collective-permute-start | bytes 1179656 | tf_op jit(solution)/shard_map/ppermute | solution.py:42
  60.6 0.1 collective-permute-start.27
  60.8 5.1 %collective-permute-start.17 = (f32[4,48,256]{2,1,0:T(8,128)S(1)}, f32[4,48,256]{2,1,0:T(8,128)S(1)}, u32[]{:S(2)}, u32[]{:S(2)}) collective-permute-start(f32[4,48,256]{2,1,0:T(8,128)S(1)} %pad_maximum_fusion.2.c0), channel_id=1, source_target_pairs={{0,192},{16,208},{32,224},{48,240},{64,128},{80,144},{96,160},{112... | collective-permute-start | bytes 589832 | tf_op jit(solution)/shard_map/ppermute | solution.py:32
  65.9 0.5 collective-permute-start.16
  66.4 0.2 collective-permute-start.15
  66.6 0.1 stack.85.place_ref
  66.7 2.4 %shard_map.50 = (f32[512,256]{1,0:T(8,128)S(1)}, f32[512,512]{1,0:T(8,128)S(1)}) custom-call(s32[7]{0:T(128)S(1)} %stack.85.place_ref, f32[4,64,256]{2,1,0:T(8,128)S(1)} %pad_maximum_fusion.1.own_ref, f32[4,64,256]{2,1,0:T(8,128)S(1)} %collective-permute-done.27.other_ref), custom_call_target="tpu_custom_call" | custom-call | tf_op jit(solution)/shard_map/pallas_call | solution.py:243
  69.1 11.4 %shard_map.51.in_ref = f32[512,512]{1,0:T(8,128)S(1)} custom-call(f32[512,512]{1,0:T(8,128)S(1)} %get-tuple-element.8.in_ref), custom_call_target="tpu_custom_call" | custom-call | tf_op jit(solution)/shard_map/pallas_call | solution.py:243
  80.5 11.0 %shard_map.52.inverse_ref = f32[512,512]{1,0:T(8,128)S(1)} custom-call(f32[512,512]{1,0:T(8,128)S(1)} %shard_map.51.in_ref), custom_call_target="tpu_custom_call" | custom-call | tf_op jit(solution)/shard_map/pallas_call | solution.py:243
  91.6 12.5 %shard_map.53 = (f32[768,512]{1,0:T(8,128)}, f32[4,2,48,256]{3,2,1,0:T(8,128)S(1)}, f32[4,2,48,256]{3,2,1,0:T(8,128)S(1)}) custom-call(s32[7]{0:T(128)S(1)} %stack.85.place_ref, f32[4,2,48,256]{3,2,1,0:T(8,128)S(1)} %pad_maximum_fusion.own_rows, f32[4,2,48,256]{3,2,1,0:T(8,128)S(1)} %collective-permute-done.10.other_rows, ...), custom_call_target="tpu_custom_call" | custom-call | tf_op jit(solution)/shard_map/pallas_call | solution.py:243
  104.0 2.8 %collective-permute-start.28 = (f32[4,2,48,256]{3,2,1,0:T(8,128)S(1)}, f32[4,2,48,256]{3,2,1,0:T(8,128)S(1)}, u32[]{:S(2)}, u32[]{:S(2)}) collective-permute-start(f32[4,2,48,256]{3,2,1,0:T(8,128)S(1)} %get-tuple-element.11), channel_id=1, source_target_pairs={{0,1},{1,0},{2,3},{3,2},{4,5},{5,4},{6,7},{7,6},{8,9},{9,8},{10,11... | collective-permute-start | bytes 1179656 | tf_op jit(solution)/shard_map/ppermute | solution.py:42
  106.9 1.3 %collective-permute-done.28 = f32[4,2,48,256]{3,2,1,0:T(8,128)S(1)} collective-permute-done((f32[4,2,48,256]{3,2,1,0:T(8,128)S(1)}, f32[4,2,48,256]{3,2,1,0:T(8,128)S(1)}, u32[]{:S(2)}, u32[]{:S(2)}) %collective-permute-start.28) | collective-permute-done | bytes 393248 | tf_op jit(solution)/shard_map/ppermute | solution.py:42
  108.2 0.1 add.120
  108.3 2.1 %collective-permute-start.30 = (f32[2,48,256]{2,1,0:T(8,128)S(1)}, f32[2,48,256]{2,1,0:T(8,128)S(1)}, u32[]{:S(2)}, u32[]{:S(2)}) collective-permute-start(f32[2,48,256]{2,1,0:T(8,128)S(1)} %get-tuple-element.16), channel_id=1, source_target_pairs={{0,4},{1,5},{2,6},{3,7},{4,0},{5,1},{6,2},{7,3},{8,12},{9,13},{10,... | collective-permute-start | bytes 294920 | tf_op jit(solution)/shard_map/ppermute | solution.py:42
  110.4 1.0 collective-permute-start.31
  111.5 2.4 %collective-permute-done.30 = f32[2,48,256]{2,1,0:T(8,128)S(1)} collective-permute-done((f32[2,48,256]{2,1,0:T(8,128)S(1)}, f32[2,48,256]{2,1,0:T(8,128)S(1)}, u32[]{:S(2)}, u32[]{:S(2)}) %collective-permute-start.30) | collective-permute-done | bytes 98336 | tf_op jit(solution)/shard_map/ppermute | solution.py:42
  113.9 2.2 %collective-permute-done.31 = f32[2,48,256]{2,1,0:T(8,128)S(1)} collective-permute-done((f32[2,48,256]{2,1,0:T(8,128)S(1)}, f32[2,48,256]{2,1,0:T(8,128)S(1)}, u32[]{:S(2)}, u32[]{:S(2)}) %collective-permute-start.31) | collective-permute-done | bytes 98336 | tf_op jit(solution)/shard_map/ppermute | solution.py:42
  116.1 5.8 %collective-permute-start.32 = (f32[48,256]{1,0:T(8,128)S(1)}, f32[48,256]{1,0:T(8,128)S(1)}, u32[]{:S(2)}, u32[]{:S(2)}) collective-permute-start(f32[48,256]{1,0:T(8,128)S(1)} %slice_bitcast_fusion.4), channel_id=1, source_target_pairs={{0,8},{1,9},{2,10},{3,11},{4,12},{5,13},{6,14},{7,15},{8,0},{9,1},... | collective-permute-start | bytes 147464 | tf_op jit(solution)/shard_map/ppermute | solution.py:42
  121.9 1.5 %collective-permute-done.32 = f32[48,256]{1,0:T(8,128)S(1)} collective-permute-done((f32[48,256]{1,0:T(8,128)S(1)}, f32[48,256]{1,0:T(8,128)S(1)}, u32[]{:S(2)}, u32[]{:S(2)}) %collective-permute-start.32) | collective-permute-done | bytes 49184 | tf_op jit(solution)/shard_map/ppermute | solution.py:42
  123.4 0.6 fusion.1
  (44 shorter events, 0.3 us)
Async XLA Ops:
  7.5 11.9 %collective-permute-start.2 = (f32[4,48,256]{2,1,0:T(8,128)S(1)}, f32[4,48,256]{2,1,0:T(8,128)S(1)}, u32[]{:S(2)}, u32[]{:S(2)}) collective-permute-start(f32[4,48,256]{2,1,0:T(8,128)S(1)} %bitcast.65), channel_id=1, source_target_pairs={{0,192},{16,208},{32,224},{48,240},{64,128},{80,144},{96,160},{112... | collective-permute-start | bytes 589832 | tf_op jit(solution)/shard_map/ppermute | solution.py:32
  11.1 8.3 %collective-permute-start.1 = (f32[4,48,256]{2,1,0:T(8,128)S(1)}, f32[4,48,256]{2,1,0:T(8,128)S(1)}, u32[]{:S(2)}, u32[]{:S(2)}) collective-permute-start(f32[4,48,256]{2,1,0:T(8,128)S(1)} %bitcast.64), channel_id=1, source_target_pairs={{0,128},{16,144},{32,160},{48,176},{64,192},{80,208},{96,224},{112... | collective-permute-start | bytes 589832 | tf_op jit(solution)/shard_map/ppermute | solution.py:32
  11.5 8.0 %collective-permute-start = (f32[4,48,256]{2,1,0:T(8,128)S(1)}, f32[4,48,256]{2,1,0:T(8,128)S(1)}, u32[]{:S(2)}, u32[]{:S(2)}) collective-permute-start(f32[4,48,256]{2,1,0:T(8,128)S(1)} %bitcast.63), channel_id=1, source_target_pairs={{0,64},{16,80},{32,96},{48,112},{64,0},{80,16},{96,32},{112,48},{1... | collective-permute-start | bytes 589832 | tf_op jit(solution)/shard_map/ppermute | solution.py:32
  19.5 72.0 %copy-start = (f32[768,256]{1,0:T(8,128)S(1)}, f32[768,256]{1,0:T(8,128)}, u32[]{:S(2)}) copy-start(f32[768,256]{1,0:T(8,128)} %targets_ref.1) | copy-start | bytes 2359300
  19.5 8.4 %collective-permute-start.4 = (f32[48,256]{1,0:T(8,128)S(1)}, f32[48,256]{1,0:T(8,128)S(1)}, u32[]{:S(2)}, u32[]{:S(2)}) collective-permute-start(f32[48,256]{1,0:T(8,128)S(1)} %get-tuple-element.19), channel_id=1, source_target_pairs={{0,32},{16,48},{32,0},{48,16},{64,96},{80,112},{96,64},{112,80},{1... | collective-permute-start | bytes 147464 | tf_op jit(solution)/shard_map/ppermute | solution.py:32
  23.5 5.3 %collective-permute-start.5 = (f32[48,256]{1,0:T(8,128)S(1)}, f32[48,256]{1,0:T(8,128)S(1)}, u32[]{:S(2)}, u32[]{:S(2)}) collective-permute-start(f32[48,256]{1,0:T(8,128)S(1)} %get-tuple-element.20), channel_id=1, source_target_pairs={{0,48},{16,32},{32,16},{48,0},{64,112},{80,96},{96,80},{112,64},{1... | collective-permute-start | bytes 147464 | tf_op jit(solution)/shard_map/ppermute | solution.py:32
  24.9 3.8 %collective-permute-start.3 = (f32[48,256]{1,0:T(8,128)S(1)}, f32[48,256]{1,0:T(8,128)S(1)}, u32[]{:S(2)}, u32[]{:S(2)}) collective-permute-start(f32[48,256]{1,0:T(8,128)S(1)} %get-tuple-element.21), channel_id=1, source_target_pairs={{0,16},{16,0},{32,48},{48,32},{64,80},{80,64},{96,112},{112,96},{1... | collective-permute-start | bytes 147464 | tf_op jit(solution)/shard_map/ppermute | solution.py:32
  25.1 9.3 %collective-permute-start.20 = (f32[64,256]{1,0:T(8,128)S(1)}, f32[64,256]{1,0:T(8,128)S(1)}, u32[]{:S(2)}, u32[]{:S(2)}) collective-permute-start(f32[64,256]{1,0:T(8,128)S(1)} %slice.84), channel_id=1, source_target_pairs={{0,192},{16,208},{32,224},{48,240},{64,128},{80,144},{96,160},{112... | collective-permute-start | bytes 196616 | tf_op jit(solution)/shard_map/ppermute | solution.py:32
  27.8 6.6 %collective-permute-start.19 = (f32[64,256]{1,0:T(8,128)S(1)}, f32[64,256]{1,0:T(8,128)S(1)}, u32[]{:S(2)}, u32[]{:S(2)}) collective-permute-start(f32[64,256]{1,0:T(8,128)S(1)} %slice.84), channel_id=1, source_target_pairs={{0,128},{16,144},{32,160},{48,176},{64,192},{80,208},{96,224},{112... | collective-permute-start | bytes 196616 | tf_op jit(solution)/shard_map/ppermute | solution.py:32
  27.9 6.5 %collective-permute-start.18 = (f32[64,256]{1,0:T(8,128)S(1)}, f32[64,256]{1,0:T(8,128)S(1)}, u32[]{:S(2)}, u32[]{:S(2)}) collective-permute-start(f32[64,256]{1,0:T(8,128)S(1)} %slice.84), channel_id=1, source_target_pairs={{0,64},{16,80},{32,96},{48,112},{64,0},{80,16},{96,32},{112,48},{1... | collective-permute-start | bytes 196616 | tf_op jit(solution)/shard_map/ppermute | solution.py:32
  28.8 15.3 %collective-permute-start.6 = (f32[48,256]{1,0:T(8,128)S(1)}, f32[48,256]{1,0:T(8,128)S(1)}, u32[]{:S(2)}, u32[]{:S(2)}) collective-permute-start(f32[48,256]{1,0:T(8,128)S(1)} %fusion.2), channel_id=1, source_target_pairs={{0,8},{1,9},{2,10},{3,11},{4,12},{5,13},{6,14},{7,15},{8,0},{9,1},... | collective-permute-start | bytes 147464 | tf_op jit(solution)/shard_map/ppermute | solution.py:42
  34.4 13.3 %collective-permute-start.23 = (f32[64,256]{1,0:T(8,128)S(1)}, f32[64,256]{1,0:T(8,128)S(1)}, u32[]{:S(2)}, u32[]{:S(2)}) collective-permute-start(f32[64,256]{1,0:T(8,128)S(1)} %add_add_fusion.2), channel_id=1, source_target_pairs={{0,48},{16,32},{32,16},{48,0},{64,112},{80,96},{96,80},{112,64},{1... | collective-permute-start | bytes 196616 | tf_op jit(solution)/shard_map/ppermute | solution.py:32
  36.1 13.1 %collective-permute-start.22 = (f32[64,256]{1,0:T(8,128)S(1)}, f32[64,256]{1,0:T(8,128)S(1)}, u32[]{:S(2)}, u32[]{:S(2)}) collective-permute-start(f32[64,256]{1,0:T(8,128)S(1)} %add_add_fusion.2), channel_id=1, source_target_pairs={{0,32},{16,48},{32,0},{48,16},{64,96},{80,112},{96,64},{112,80},{1... | collective-permute-start | bytes 196616 | tf_op jit(solution)/shard_map/ppermute | solution.py:32
  36.5 12.8 %collective-permute-start.21 = (f32[64,256]{1,0:T(8,128)S(1)}, f32[64,256]{1,0:T(8,128)S(1)}, u32[]{:S(2)}, u32[]{:S(2)}) collective-permute-start(f32[64,256]{1,0:T(8,128)S(1)} %add_add_fusion.2), channel_id=1, source_target_pairs={{0,16},{16,0},{32,48},{48,32},{64,80},{80,64},{96,112},{112,96},{1... | collective-permute-start | bytes 196616 | tf_op jit(solution)/shard_map/ppermute | solution.py:32
  38.1 14.0 %collective-permute-start.11 = (f32[48,256]{1,0:T(8,128)S(1)}, f32[48,256]{1,0:T(8,128)S(1)}, u32[]{:S(2)}, u32[]{:S(2)}) collective-permute-start(f32[48,256]{1,0:T(8,128)S(1)} %fusion.2), channel_id=1, source_target_pairs={{0,0},{1,16},{2,32},{3,48},{4,64},{5,80},{6,96},{7,112},{8,128},{9... | collective-permute-start | bytes 147464 | tf_op jit(solution)/shard_map/ppermute | solution.py:47
  44.1 8.0 %collective-permute-start.8 = (f32[2,48,256]{2,1,0:T(8,128)S(1)}, f32[2,48,256]{2,1,0:T(8,128)S(1)}, u32[]{:S(2)}, u32[]{:S(2)}) collective-permute-start(f32[2,48,256]{2,1,0:T(8,128)S(1)} %get-tuple-element.23), channel_id=1, source_target_pairs={{0,4},{1,5},{2,6},{3,7},{4,0},{5,1},{6,2},{7,3},{8,12},{9,13},{10,... | collective-permute-start | bytes 294920 | tf_op jit(solution)/shard_map/ppermute | solution.py:42
  47.7 7.0 %collective-permute-start.7 = (f32[2,48,256]{2,1,0:T(8,128)S(1)}, f32[2,48,256]{2,1,0:T(8,128)S(1)}, u32[]{:S(2)}, u32[]{:S(2)}) collective-permute-start(f32[2,48,256]{2,1,0:T(8,128)S(1)} %get-tuple-element.23), channel_id=1, source_target_pairs={{0,2},{1,3},{2,0},{3,1},{4,6},{5,7},{6,4},{7,5},{8,10},{9,11},{10,... | collective-permute-start | bytes 294920 | tf_op jit(solution)/shard_map/ppermute | solution.py:42
  49.2 5.4 %collective-permute-start.9 = (f32[2,48,256]{2,1,0:T(8,128)S(1)}, f32[2,48,256]{2,1,0:T(8,128)S(1)}, u32[]{:S(2)}, u32[]{:S(2)}) collective-permute-start(f32[2,48,256]{2,1,0:T(8,128)S(1)} %get-tuple-element.23), channel_id=1, source_target_pairs={{0,6},{1,7},{2,4},{3,5},{4,2},{5,3},{6,0},{7,1},{8,14},{9,15},{10,... | collective-permute-start | bytes 294920 | tf_op jit(solution)/shard_map/ppermute | solution.py:42
  49.3 8.0 %collective-permute-start.26 = (f32[64,256]{1,0:T(8,128)S(1)}, f32[64,256]{1,0:T(8,128)S(1)}, u32[]{:S(2)}, u32[]{:S(2)}) collective-permute-start(f32[64,256]{1,0:T(8,128)S(1)} %add_add_fusion.1), channel_id=1, source_target_pairs={{0,6},{1,7},{2,4},{3,5},{4,2},{5,3},{6,0},{7,1},{8,14},{9,15},{10,... | collective-permute-start | bytes 196616 | tf_op jit(solution)/shard_map/ppermute | solution.py:42
  52.0 6.3 %collective-permute-start.25 = (f32[64,256]{1,0:T(8,128)S(1)}, f32[64,256]{1,0:T(8,128)S(1)}, u32[]{:S(2)}, u32[]{:S(2)}) collective-permute-start(f32[64,256]{1,0:T(8,128)S(1)} %add_add_fusion.1), channel_id=1, source_target_pairs={{0,4},{1,5},{2,6},{3,7},{4,0},{5,1},{6,2},{7,3},{8,12},{9,13},{10,... | collective-permute-start | bytes 196616 | tf_op jit(solution)/shard_map/ppermute | solution.py:42
  52.0 8.6 %collective-permute-start.24 = (f32[64,256]{1,0:T(8,128)S(1)}, f32[64,256]{1,0:T(8,128)S(1)}, u32[]{:S(2)}, u32[]{:S(2)}) collective-permute-start(f32[64,256]{1,0:T(8,128)S(1)} %add_add_fusion.1), channel_id=1, source_target_pairs={{0,2},{1,3},{2,0},{3,1},{4,6},{5,7},{6,4},{7,5},{8,10},{9,11},{10,... | collective-permute-start | bytes 196616 | tf_op jit(solution)/shard_map/ppermute | solution.py:42
  54.7 6.1 %collective-permute-start.14 = (f32[48,256]{1,0:T(8,128)S(1)}, f32[48,256]{1,0:T(8,128)S(1)}, u32[]{:S(2)}, u32[]{:S(2)}) collective-permute-start(f32[48,256]{1,0:T(8,128)S(1)} %collective-permute-done.11), channel_id=1, source_target_pairs={{0,48},{16,32},{32,16},{48,0},{64,112},{80,96},{96,80},{112,64},{1... | collective-permute-start | bytes 147464 | tf_op jit(solution)/shard_map/ppermute | solution.py:32
  54.7 6.1 %collective-permute-start.13 = (f32[48,256]{1,0:T(8,128)S(1)}, f32[48,256]{1,0:T(8,128)S(1)}, u32[]{:S(2)}, u32[]{:S(2)}) collective-permute-start(f32[48,256]{1,0:T(8,128)S(1)} %collective-permute-done.11), channel_id=1, source_target_pairs={{0,32},{16,48},{32,0},{48,16},{64,96},{80,112},{96,64},{112,80},{1... | collective-permute-start | bytes 147464 | tf_op jit(solution)/shard_map/ppermute | solution.py:32
  57.3 3.5 %collective-permute-start.12 = (f32[48,256]{1,0:T(8,128)S(1)}, f32[48,256]{1,0:T(8,128)S(1)}, u32[]{:S(2)}, u32[]{:S(2)}) collective-permute-start(f32[48,256]{1,0:T(8,128)S(1)} %collective-permute-done.11), channel_id=1, source_target_pairs={{0,16},{16,0},{32,48},{48,32},{64,80},{80,64},{96,112},{112,96},{1... | collective-permute-start | bytes 147464 | tf_op jit(solution)/shard_map/ppermute | solution.py:32
  58.3 33.2 %collective-permute-start.10 = (f32[4,2,48,256]{3,2,1,0:T(8,128)S(1)}, f32[4,2,48,256]{3,2,1,0:T(8,128)S(1)}, u32[]{:S(2)}, u32[]{:S(2)}) collective-permute-start(f32[4,2,48,256]{3,2,1,0:T(8,128)S(1)} %pad_maximum_fusion.own_rows), channel_id=1, source_target_pairs={{0,1},{1,0},{2,3},{3,2},{4,5},{5,4},{6,7},{7,6},{8,9},{9,8},{10,11... | collective-permute-start | bytes 1179656 | tf_op jit(solution)/shard_map/ppermute | solution.py:42
  60.6 6.0 %collective-permute-start.27 = (f32[4,64,256]{2,1,0:T(8,128)S(1)}, f32[4,64,256]{2,1,0:T(8,128)S(1)}, u32[]{:S(2)}, u32[]{:S(2)}) collective-permute-start(f32[4,64,256]{2,1,0:T(8,128)S(1)} %pad_maximum_fusion.1.own_ref), channel_id=1, source_target_pairs={{0,1},{1,0},{2,3},{3,2},{4,5},{5,4},{6,7},{7,6},{8,9},{9,8},{10,11... | collective-permute-start | bytes 786440 | tf_op jit(solution)/shard_map/ppermute | solution.py:42
  60.8 30.7 %collective-permute-start.17 = (f32[4,48,256]{2,1,0:T(8,128)S(1)}, f32[4,48,256]{2,1,0:T(8,128)S(1)}, u32[]{:S(2)}, u32[]{:S(2)}) collective-permute-start(f32[4,48,256]{2,1,0:T(8,128)S(1)} %pad_maximum_fusion.2.c0), channel_id=1, source_target_pairs={{0,192},{16,208},{32,224},{48,240},{64,128},{80,144},{96,160},{112... | collective-permute-start | bytes 589832 | tf_op jit(solution)/shard_map/ppermute | solution.py:32
  65.9 25.6 %collective-permute-start.16 = (f32[4,48,256]{2,1,0:T(8,128)S(1)}, f32[4,48,256]{2,1,0:T(8,128)S(1)}, u32[]{:S(2)}, u32[]{:S(2)}) collective-permute-start(f32[4,48,256]{2,1,0:T(8,128)S(1)} %pad_maximum_fusion.2.c0), channel_id=1, source_target_pairs={{0,128},{16,144},{32,160},{48,176},{64,192},{80,208},{96,224},{112... | collective-permute-start | bytes 589832 | tf_op jit(solution)/shard_map/ppermute | solution.py:32
  66.4 25.1 %collective-permute-start.15 = (f32[4,48,256]{2,1,0:T(8,128)S(1)}, f32[4,48,256]{2,1,0:T(8,128)S(1)}, u32[]{:S(2)}, u32[]{:S(2)}) collective-permute-start(f32[4,48,256]{2,1,0:T(8,128)S(1)} %pad_maximum_fusion.2.c0), channel_id=1, source_target_pairs={{0,64},{16,80},{32,96},{48,112},{64,0},{80,16},{96,32},{112,48},{1... | collective-permute-start | bytes 589832 | tf_op jit(solution)/shard_map/ppermute | solution.py:32
  104.0 4.2 %collective-permute-start.28 = (f32[4,2,48,256]{3,2,1,0:T(8,128)S(1)}, f32[4,2,48,256]{3,2,1,0:T(8,128)S(1)}, u32[]{:S(2)}, u32[]{:S(2)}) collective-permute-start(f32[4,2,48,256]{3,2,1,0:T(8,128)S(1)} %get-tuple-element.11), channel_id=1, source_target_pairs={{0,1},{1,0},{2,3},{3,2},{4,5},{5,4},{6,7},{7,6},{8,9},{9,8},{10,11... | collective-permute-start | bytes 1179656 | tf_op jit(solution)/shard_map/ppermute | solution.py:42
  108.3 5.6 %collective-permute-start.30 = (f32[2,48,256]{2,1,0:T(8,128)S(1)}, f32[2,48,256]{2,1,0:T(8,128)S(1)}, u32[]{:S(2)}, u32[]{:S(2)}) collective-permute-start(f32[2,48,256]{2,1,0:T(8,128)S(1)} %get-tuple-element.16), channel_id=1, source_target_pairs={{0,4},{1,5},{2,6},{3,7},{4,0},{5,1},{6,2},{7,3},{8,12},{9,13},{10,... | collective-permute-start | bytes 294920 | tf_op jit(solution)/shard_map/ppermute | solution.py:42
  110.4 5.6 %collective-permute-start.31 = (f32[2,48,256]{2,1,0:T(8,128)S(1)}, f32[2,48,256]{2,1,0:T(8,128)S(1)}, u32[]{:S(2)}, u32[]{:S(2)}) collective-permute-start(f32[2,48,256]{2,1,0:T(8,128)S(1)} %get-tuple-element.17), channel_id=1, source_target_pairs={{0,6},{1,7},{2,4},{3,5},{4,2},{5,3},{6,0},{7,1},{8,14},{9,15},{10,... | collective-permute-start | bytes 294920 | tf_op jit(solution)/shard_map/ppermute | solution.py:42
  111.5 4.6 %collective-permute-start.29 = (f32[2,48,256]{2,1,0:T(8,128)S(1)}, f32[2,48,256]{2,1,0:T(8,128)S(1)}, u32[]{:S(2)}, u32[]{:S(2)}) collective-permute-start(f32[2,48,256]{2,1,0:T(8,128)S(1)} %get-tuple-element.18), channel_id=1, source_target_pairs={{0,2},{1,3},{2,0},{3,1},{4,6},{5,7},{6,4},{7,5},{8,10},{9,11},{10,... | collective-permute-start | bytes 294920 | tf_op jit(solution)/shard_map/ppermute | solution.py:42
  116.1 7.3 %collective-permute-start.32 = (f32[48,256]{1,0:T(8,128)S(1)}, f32[48,256]{1,0:T(8,128)S(1)}, u32[]{:S(2)}, u32[]{:S(2)}) collective-permute-start(f32[48,256]{1,0:T(8,128)S(1)} %slice_bitcast_fusion.4), channel_id=1, source_target_pairs={{0,8},{1,9},{2,10},{3,11},{4,12},{5,13},{6,14},{7,15},{8,0},{9,1},... | collective-permute-start | bytes 147464 | tf_op jit(solution)/shard_map/ppermute | solution.py:42
where the time goes:
time: 126 us; the launch traced here: 124 us
  starting transfers between devices  60.4 us (48%)
  Pallas kernels  37.3 us (30%)
  waiting for transfers between devices  17.6 us (14%)
  local copies, waits for them, and re-layouts  6.3 us (5%)
  other arithmetic  1.4 us (1%)
    pallas_call x4, Pallas kernels, call(): pl.pallas_call(kernel, out_shape=tuple((s if far else pltpu.VMEM(s.shape,...  37.3 us
    ppermute x14, starting transfers between devices, col_swap(): return lax.ppermute(value, 'col', pairs)  28.6 us
    ppermute x18, starting transfers between devices, row_swap(): return lax.ppermute(value, 'row', pairs)  25.8 us
    ppermute x14, waiting for transfers between devices, col_swap(): return lax.ppermute(value, 'col', pairs)  9.69 us
    ppermute x18, waiting for transfers between devices, row_swap(): return lax.ppermute(value, 'row', pairs)  7.91 us
    ppermute x1, starting transfers between devices, flip(): return lax.ppermute(value, ('row', 'col'), pairs)  5.97 us
    gather x1, local copies, waits for them, and re-layouts, per_device(): picked = jnp.take(archive, jnp.clip(ids, 0, shard - 1), axis=0)  4.87 us
  transfers between devices with their start and end apart: 33, of which 8 were waited for; matrix products, arithmetic and copies ran while one was open for 0% of the time, Pallas kernels for 20%

commit v1 on v0

--- a/solution.py
+++ b/solution.py
@@ -22,7 +22,6 @@
 HALF = LOCAL // 2
 ROUND = 8
 
-precise = lax.Precision.HIGHEST
 nugget = 1.0
 scale = 5.0**0.5 / 16.0
 
@@ -47,12 +46,11 @@
     return lax.ppermute(value, ("row", "col"), pairs)
 
 
-def dot(left, right, left_dim, right_dim, precision=None):
+def dot(left, right, left_dim, right_dim):
     return lax.dot_general(
         left,
         right,
         (((left_dim,), (right_dim,)), ((), ())),
-        precision=precision,
         preferred_element_type=jnp.float32,
     )
 
@@ -71,9 +69,13 @@
 
 
 def lane_squares(value):
-    square = value * value
-    ones = jnp.ones((8, square.shape[1]), jnp.float32)
-    return dot(ones, square, 1, 1, precise)[0:1, :]
+    rest, total = value * value, 0.0
+    ones = jnp.ones((16, value.shape[1]), jnp.bfloat16)
+    for _ in range(3):
+        term = rest.astype(jnp.bfloat16)
+        rest = rest - term.astype(jnp.float32)
+        total = total + dot(ones, term, 1, 1)
+    return total[0:1, :]
 
 
 def matern(left_sq, right_sq, cross):
@@ -139,7 +141,7 @@
         lead_ref[pl.ds(aligned((at + 1 - k) * LEAD_PIECE), LEAD_PIECE), :] = other_ref[s] * scale
     lead = lead_ref[...]
     left_sq = jnp.sum(lead * lead, axis=1, keepdims=True)
-    block = matern(left_sq, lane_squares(lead), dot(lead, lead * -2.0, 1, 1, precise))
+    block = matern(left_sq, lane_squares(lead), dot3(split(lead), split(lead * -2.0), 1, 1))
     row = lax.broadcasted_iota(jnp.int32, (LEAD, LEAD), 0)
     lane = lax.broadcasted_iota(jnp.int32, (LEAD, LEAD), 1)
     out_ref[...] = block + jnp.where(row == lane, nugget, 0.0)
@@ -155,13 +157,14 @@
         here = pl.ds(off, 128)
         inverse = eliminate([out_ref[pl.ds(off + 8 * v, 8), here] for v in range(16)])
         later = tall >= off + 128
-        below = jnp.where(later, dot(out_ref[first:, here], inverse, 1, 1, precise), 0.0)
-        across = dot(inverse, out_ref[here, :], 1, 0, precise)
+        pair = split(inverse)
+        below = jnp.where(later, dot3(split(out_ref[first:, here]), pair, 1, 1), 0.0)
+        across = dot3(pair, split(out_ref[here, :]), 1, 0)
         out_ref[first:, here] = jnp.where(later, 0.0, out_ref[first:, here])
         out_ref[here, :] = across
         out_ref[here, here] = inverse
         across = out_ref[here, :]
-        out_ref[first:, :] = out_ref[first:, :] - dot(below, across, 1, 0, precise)
+        out_ref[first:, :] = out_ref[first:, :] - dot3(split(below), split(across), 1, 0)
         out_ref[here, :] = jnp.where(wide < off + 128, across, 0.0)
         return carry
 
@@ -171,7 +174,7 @@
 def slab_kernel(
     place_ref, own_rows, other_rows, c0, c1, c2, c3, lead_ref, inverse_ref, targets_ref,
     panel_ref, part_other_ref, part_own_ref,
-    left_ref, sum_ref, cols_ref, cols_high, cols_low, goal_high, goal_low, lead_high, lead_low, inv_high, inv_low,
+    left_ref, cols_ref, cols_high, cols_low, goal_high, goal_low, lead_high, lead_low, inv_high, inv_low,
 ):
     y, z, h, x, k, row_place, col_place = (place_ref[i] for i in range(7))
     for a, ref in enumerate((c0, c1, c2, c3)):
@@ -196,16 +199,14 @@
     weights = split(dot3(whole(inv), split(gram), 1, 0))
     same = jnp.where(row_place == col_place, nugget, 0.0)
 
+    def starts_of(core):
+        return [aligned((((h ^ e) * 4 + (x ^ s)) * 2 + core) * PIECE) for s in range(4) for e in range(2)]
+
     def panel_step(side, carry):
-        core = jnp.where(side == 0, 1 - k, k)
-        where = pl.ds(aligned(side * HALF), HALF)
-        starts = [
-            aligned((((h ^ e) * 4 + (x ^ s)) * 2 + core) * PIECE) for s in range(4) for e in range(2)
-        ]
-        left = left_ref[where, :]
+        starts = starts_of(jnp.where(side == 0, 1 - k, k))
+        left = left_ref[pl.ds(aligned(side * HALF), HALF), :]
         left_sq = jnp.sum(left * left, axis=1, keepdims=True)
-        pair = split(left)
-        block = matern(left_sq, lead_lane, dot3(pair, whole(lead), 1, 1))
+        block = matern(left_sq, lead_lane, dot3(split(left), whole(lead), 1, 1))
         row = jnp.concatenate([lax.broadcasted_iota(jnp.int32, (PIECE, 1), 0) + start for start in starts], axis=0)
         spot = jnp.where(row < NB, row + row_place * NB, LEAD)
         lane = lax.broadcasted_iota(jnp.int32, (HALF, LEAD), 1)
@@ -213,14 +214,19 @@
         panel = dot3(split(block), whole(inv), 1, 1)
         for n, start in enumerate(starts):
             panel_ref[pl.ds(start, PIECE), :] = panel[n * PIECE : n * PIECE + PIECE]
-        block = matern(left_sq, col_lane, dot3(pair, whole(cols), 1, 1))
+        return carry
+
+    lax.fori_loop(0, 2, panel_step, 0)
+
+    for side, part_ref in enumerate((part_other_ref, part_own_ref)):
+        starts = starts_of((1 - k, k)[side])
+        left = left_ref[side * HALF : side * HALF + HALF, :]
+        left_sq = jnp.sum(left * left, axis=1, keepdims=True)
+        block = matern(left_sq, col_lane, dot3(split(left), whole(cols), 1, 1))
+        panel = jnp.concatenate([panel_ref[pl.ds(start, PIECE), :] for start in starts], axis=0)
         diag = jnp.concatenate([targets_ref[pl.ds(start, PIECE), :] for start in starts], axis=0)
-        sum_ref[where, :] = dot3(split(block), whole(goal), 1, 0) + diag * same - dot3(split(panel), weights, 1, 0)
-        return carry
-
-    lax.fori_loop(0, 2, panel_step, 0)
-    part_other_ref[...] = sum_ref[:HALF, :].reshape(4, 2, PIECE, NT)
-    part_own_ref[...] = sum_ref[HALF:, :].reshape(4, 2, PIECE, NT)
+        total = dot3(split(block), whole(goal), 1, 0) + diag * same - dot3(split(panel), weights, 1, 0)
+        part_ref[...] = total.reshape(4, 2, PIECE, NT)
 
 
 def per_device(archive, slab_index, targets):
@@ -301,7 +307,7 @@
             (array(f32, 4, 2, PIECE, NT), False),
             (array(f32, 4, 2, PIECE, NT), False),
         ),
-        (array(f32, LOCAL, F), array(f32, LOCAL, NT), array(f32, LOCAL, F))
+        (array(f32, LOCAL, F), array(f32, LOCAL, F))
         + (array(bf16, LOCAL, F),) * 4
         + (array(bf16, LEAD, F),) * 2
         + (array(bf16, LEAD, LEAD),) * 2,

time: 126 us -> 122 us (0.968)
  Pallas kernels: 37.3 us -> 33.6 us
    pallas_call x4, Pallas kernels: 37.3 us -> 33.6 us  [call(): pl.pallas_call(kernel, out_shape=tuple((s if far else pltpu.VMEM(s.shape,...]
  transfers between devices with their start and end apart: 33 -> 33, of which waited for: 8 -> 8; matrix products, arithmetic and copies ran while one was open for 0% -> 0% of each run, Pallas kernels for 20% -> 18%
where the time goes in v1:
time: 122 us; the launch traced here: 120 us
  starting transfers between devices  60.4 us (50%)
  Pallas kernels  33.6 us (28%)
  waiting for transfers between devices  17.6 us (14%)
  local copies, waits for them, and re-layouts  6.3 us (5%)
  other arithmetic  1.4 us (1%)
    pallas_call x4, Pallas kernels, call(): pl.pallas_call(kernel, out_shape=tuple((s if far else pltpu.VMEM(s.shape,...  33.6 us
    ppermute x14, starting transfers between devices, col_swap(): return lax.ppermute(value, 'col', pairs)  28.6 us
    ppermute x18, starting transfers between devices, row_swap(): return lax.ppermute(value, 'row', pairs)  25.8 us
    ppermute x14, waiting for transfers between devices, col_swap(): return lax.ppermute(value, 'col', pairs)  9.67 us
    ppermute x18, waiting for transfers between devices, row_swap(): return lax.ppermute(value, 'row', pairs)  7.91 us
    ppermute x1, starting transfers between devices, flip(): return lax.ppermute(value, ('row', 'col'), pairs)  5.97 us
    gather x1, local copies, waits for them, and re-layouts, per_device(): picked = jnp.take(archive, jnp.clip(ids, 0, shard - 1), axis=0)  4.87 us
  transfers between devices with their start and end apart: 33, of which 8 were waited for; matrix products, arithmetic and copies ran while one was open for 0% of the time, Pallas kernels for 18%

profile of v1, /device:TPU:1, one launch (start us, length us, event | category | flops | bytes accessed | tf_op | source)
XLA Modules:
  0.0 120.3 jit_solution(16720698885112406948)
XLA Ops:
  0.7 0.8 reshape.92
  1.6 0.1 dynamic-slice_bitcast_fusion
  1.7 0.1 dynamic_slice.6
  1.7 0.1 constant_dynamic-slice_fusion
  1.9 0.1 concatenate.26
  2.0 0.1 concatenate.23
  2.1 0.1 fusion.3
  2.2 0.1 compare_and_fusion.1
  2.3 4.9 %gather_fusion = f32[832,256]{1,0:T(8,128)S(1)} fusion(f32[4096,256]{1,0:T(8,128)} %param.3, s32[1024]{0:T(1024)S(1)} %pad_clamp_fusion), kind=kCustom, calls=%fused_computation | custom fusion | bytes 1707264 | tf_op jit(solution)/shard_map/jit(_take)/gather | solution.py:273
  7.1 0.3 select_select_fusion
  7.4 0.1 fusion.6
  7.5 3.6 %collective-permute-start.2 = (f32[4,48,256]{2,1,0:T(8,128)S(1)}, f32[4,48,256]{2,1,0:T(8,128)S(1)}, u32[]{:S(2)}, u32[]{:S(2)}) collective-permute-start(f32[4,48,256]{2,1,0:T(8,128)S(1)} %bitcast.65), channel_id=1, source_target_pairs={{0,192},{16,208},{32,224},{48,240},{64,128},{80,144},{96,160},{112... | collective-permute-start | bytes 589832 | tf_op jit(solution)/shard_map/ppermute | solution.py:31
  11.1 0.3 collective-permute-start.1
  11.5 0.3 collective-permute-start
  11.8 7.6 %collective-permute-done.2 = f32[4,48,256]{2,1,0:T(8,128)S(1)} collective-permute-done((f32[4,48,256]{2,1,0:T(8,128)S(1)}, f32[4,48,256]{2,1,0:T(8,128)S(1)}, u32[]{:S(2)}, u32[]{:S(2)}) %collective-permute-start.2) | collective-permute-done | bytes 196640 | tf_op jit(solution)/shard_map/ppermute | solution.py:31
  19.4 0.0 collective-permute-done.1
  19.4 0.0 collective-permute-done
  19.4 0.1 add_add_fusion
  19.5 0.0 copy-start
  19.5 3.9 %collective-permute-start.4 = (f32[48,256]{1,0:T(8,128)S(1)}, f32[48,256]{1,0:T(8,128)S(1)}, u32[]{:S(2)}, u32[]{:S(2)}) collective-permute-start(f32[48,256]{1,0:T(8,128)S(1)} %get-tuple-element.19), channel_id=1, source_target_pairs={{0,32},{16,48},{32,0},{48,16},{64,96},{80,112},{96,64},{112,80},{1... | collective-permute-start | bytes 147464 | tf_op jit(solution)/shard_map/ppermute | solution.py:31
  23.5 1.5 %collective-permute-start.5 = (f32[48,256]{1,0:T(8,128)S(1)}, f32[48,256]{1,0:T(8,128)S(1)}, u32[]{:S(2)}, u32[]{:S(2)}) collective-permute-start(f32[48,256]{1,0:T(8,128)S(1)} %get-tuple-element.20), channel_id=1, source_target_pairs={{0,48},{16,32},{32,16},{48,0},{64,112},{80,96},{96,80},{112,64},{1... | collective-permute-start | bytes 147464 | tf_op jit(solution)/shard_map/ppermute | solution.py:31
  24.9 0.2 collective-permute-start.3
  25.1 2.7 %collective-permute-start.20 = (f32[64,256]{1,0:T(8,128)S(1)}, f32[64,256]{1,0:T(8,128)S(1)}, u32[]{:S(2)}, u32[]{:S(2)}) collective-permute-start(f32[64,256]{1,0:T(8,128)S(1)} %slice.84), channel_id=1, source_target_pairs={{0,192},{16,208},{32,224},{48,240},{64,128},{80,144},{96,160},{112... | collective-permute-start | bytes 196616 | tf_op jit(solution)/shard_map/ppermute | solution.py:31
  27.8 0.1 collective-permute-start.19
  27.9 0.0 collective-permute-done.4
  27.9 0.6 collective-permute-start.18
  28.5 0.2 collective-permute-done.5
  28.8 5.6 %collective-permute-start.6 = (f32[48,256]{1,0:T(8,128)S(1)}, f32[48,256]{1,0:T(8,128)S(1)}, u32[]{:S(2)}, u32[]{:S(2)}) collective-permute-start(f32[48,256]{1,0:T(8,128)S(1)} %fusion.2), channel_id=1, source_target_pairs={{0,8},{1,9},{2,10},{3,11},{4,12},{5,13},{6,14},{7,15},{8,0},{9,1},... | collective-permute-start | bytes 147464 | tf_op jit(solution)/shard_map/ppermute | solution.py:41
  34.4 0.0 collective-permute-done.20
  34.4 0.0 collective-permute-done.19
  34.4 0.0 collective-permute-done.18
  34.4 1.7 %collective-permute-start.23 = (f32[64,256]{1,0:T(8,128)S(1)}, f32[64,256]{1,0:T(8,128)S(1)}, u32[]{:S(2)}, u32[]{:S(2)}) collective-permute-start(f32[64,256]{1,0:T(8,128)S(1)} %add_add_fusion.2), channel_id=1, source_target_pairs={{0,48},{16,32},{32,16},{48,0},{64,112},{80,96},{96,80},{112,64},{1... | collective-permute-start | bytes 196616 | tf_op jit(solution)/shard_map/ppermute | solution.py:31
  36.1 0.3 collective-permute-start.22
  36.5 1.6 %collective-permute-start.21 = (f32[64,256]{1,0:T(8,128)S(1)}, f32[64,256]{1,0:T(8,128)S(1)}, u32[]{:S(2)}, u32[]{:S(2)}) collective-permute-start(f32[64,256]{1,0:T(8,128)S(1)} %add_add_fusion.2), channel_id=1, source_target_pairs={{0,16},{16,0},{32,48},{48,32},{64,80},{80,64},{96,112},{112,96},{1... | collective-permute-start | bytes 196616 | tf_op jit(solution)/shard_map/ppermute | solution.py:31
  38.1 6.0 %collective-permute-start.11 = (f32[48,256]{1,0:T(8,128)S(1)}, f32[48,256]{1,0:T(8,128)S(1)}, u32[]{:S(2)}, u32[]{:S(2)}) collective-permute-start(f32[48,256]{1,0:T(8,128)S(1)} %fusion.2), channel_id=1, source_target_pairs={{0,0},{1,16},{2,32},{3,48},{4,64},{5,80},{6,96},{7,112},{8,128},{9... | collective-permute-start | bytes 147464 | tf_op jit(solution)/shard_map/ppermute | solution.py:46
  44.1 3.6 %collective-permute-start.8 = (f32[2,48,256]{2,1,0:T(8,128)S(1)}, f32[2,48,256]{2,1,0:T(8,128)S(1)}, u32[]{:S(2)}, u32[]{:S(2)}) collective-permute-start(f32[2,48,256]{2,1,0:T(8,128)S(1)} %get-tuple-element.23), channel_id=1, source_target_pairs={{0,4},{1,5},{2,6},{3,7},{4,0},{5,1},{6,2},{7,3},{8,12},{9,13},{10,... | collective-permute-start | bytes 294920 | tf_op jit(solution)/shard_map/ppermute | solution.py:41
  47.7 1.5 %collective-permute-start.7 = (f32[2,48,256]{2,1,0:T(8,128)S(1)}, f32[2,48,256]{2,1,0:T(8,128)S(1)}, u32[]{:S(2)}, u32[]{:S(2)}) collective-permute-start(f32[2,48,256]{2,1,0:T(8,128)S(1)} %get-tuple-element.23), channel_id=1, source_target_pairs={{0,2},{1,3},{2,0},{3,1},{4,6},{5,7},{6,4},{7,5},{8,10},{9,11},{10,... | collective-permute-start | bytes 294920 | tf_op jit(solution)/shard_map/ppermute | solution.py:41
  49.3 2.8 %collective-permute-start.26 = (f32[64,256]{1,0:T(8,128)S(1)}, f32[64,256]{1,0:T(8,128)S(1)}, u32[]{:S(2)}, u32[]{:S(2)}) collective-permute-start(f32[64,256]{1,0:T(8,128)S(1)} %add_add_fusion.1), channel_id=1, source_target_pairs={{0,6},{1,7},{2,4},{3,5},{4,2},{5,3},{6,0},{7,1},{8,14},{9,15},{10,... | collective-permute-start | bytes 196616 | tf_op jit(solution)/shard_map/ppermute | solution.py:41
  52.0 1.0 collective-permute-start.24
  53.0 1.6 %collective-permute-done.7 = f32[2,48,256]{2,1,0:T(8,128)S(1)} collective-permute-done((f32[2,48,256]{2,1,0:T(8,128)S(1)}, f32[2,48,256]{2,1,0:T(8,128)S(1)}, u32[]{:S(2)}, u32[]{:S(2)}) %collective-permute-start.7) | collective-permute-done | bytes 98336 | tf_op jit(solution)/shard_map/ppermute | solution.py:41
  54.7 0.0 collective-permute-start.14
  54.7 2.0 %collective-permute-start.13 = (f32[48,256]{1,0:T(8,128)S(1)}, f32[48,256]{1,0:T(8,128)S(1)}, u32[]{:S(2)}, u32[]{:S(2)}) collective-permute-start(f32[48,256]{1,0:T(8,128)S(1)} %collective-permute-done.11), channel_id=1, source_target_pairs={{0,32},{16,48},{32,0},{48,16},{64,96},{80,112},{96,64},{112,80},{1... | collective-permute-start | bytes 147464 | tf_op jit(solution)/shard_map/ppermute | solution.py:31
  56.7 0.6 collective-permute-done.26
  57.3 1.1 collective-permute-start.12
  58.3 2.3 %collective-permute-start.10 = (f32[4,2,48,256]{3,2,1,0:T(8,128)S(1)}, f32[4,2,48,256]{3,2,1,0:T(8,128)S(1)}, u32[]{:S(2)}, u32[]{:S(2)}) collective-permute-start(f32[4,2,48,256]{3,2,1,0:T(8,128)S(1)} %pad_maximum_fusion.own_rows), channel_id=1, source_target_pairs={{0,1},{1,0},{2,3},{3,2},{4,5},{5,4},{6,7},{7,6},{8,9},{9,8},{10,11... | collective-permute-start | bytes 1179656 | tf_op jit(solution)/shard_map/ppermute | solution.py:41
  60.6 0.1 collective-permute-start.27
  60.8 5.1 %collective-permute-start.17 = (f32[4,48,256]{2,1,0:T(8,128)S(1)}, f32[4,48,256]{2,1,0:T(8,128)S(1)}, u32[]{:S(2)}, u32[]{:S(2)}) collective-permute-start(f32[4,48,256]{2,1,0:T(8,128)S(1)} %pad_maximum_fusion.2.c0), channel_id=1, source_target_pairs={{0,192},{16,208},{32,224},{48,240},{64,128},{80,144},{96,160},{112... | collective-permute-start | bytes 589832 | tf_op jit(solution)/shard_map/ppermute | solution.py:31
  65.9 0.5 collective-permute-start.16
  66.4 0.2 collective-permute-start.15
  66.6 0.1 stack.85.place_ref
  66.7 1.8 %shard_map.50 = (f32[512,256]{1,0:T(8,128)S(1)}, f32[512,512]{1,0:T(8,128)S(1)}) custom-call(s32[7]{0:T(128)S(1)} %stack.85.place_ref, f32[4,64,256]{2,1,0:T(8,128)S(1)} %pad_maximum_fusion.1.own_ref, f32[4,64,256]{2,1,0:T(8,128)S(1)} %collective-permute-done.27.other_ref), custom_call_target="tpu_custom_call" | custom-call | tf_op jit(solution)/shard_map/pallas_call | solution.py:249
  68.4 10.4 %shard_map.51.in_ref = f32[512,512]{1,0:T(8,128)S(1)} custom-call(f32[512,512]{1,0:T(8,128)S(1)} %get-tuple-element.8.in_ref), custom_call_target="tpu_custom_call" | custom-call | tf_op jit(solution)/shard_map/pallas_call | solution.py:249
  78.8 9.8 %shard_map.52.inverse_ref = f32[512,512]{1,0:T(8,128)S(1)} custom-call(f32[512,512]{1,0:T(8,128)S(1)} %shard_map.51.in_ref), custom_call_target="tpu_custom_call" | custom-call | tf_op jit(solution)/shard_map/pallas_call | solution.py:249
  88.6 11.7 %shard_map.53 = (f32[768,512]{1,0:T(8,128)}, f32[4,2,48,256]{3,2,1,0:T(8,128)S(1)}, f32[4,2,48,256]{3,2,1,0:T(8,128)S(1)}) custom-call(s32[7]{0:T(128)S(1)} %stack.85.place_ref, f32[4,2,48,256]{3,2,1,0:T(8,128)S(1)} %pad_maximum_fusion.own_rows, f32[4,2,48,256]{3,2,1,0:T(8,128)S(1)} %collective-permute-done.10.other_rows, ...), custom_call_target="tpu_custom_call" | custom-call | tf_op jit(solution)/shard_map/pallas_call | solution.py:249
  100.3 2.8 %collective-permute-start.28 = (f32[4,2,48,256]{3,2,1,0:T(8,128)S(1)}, f32[4,2,48,256]{3,2,1,0:T(8,128)S(1)}, u32[]{:S(2)}, u32[]{:S(2)}) collective-permute-start(f32[4,2,48,256]{3,2,1,0:T(8,128)S(1)} %get-tuple-element.11), channel_id=1, source_target_pairs={{0,1},{1,0},{2,3},{3,2},{4,5},{5,4},{6,7},{7,6},{8,9},{9,8},{10,11... | collective-permute-start | bytes 1179656 | tf_op jit(solution)/shard_map/ppermute | solution.py:41
  103.1 1.3 %collective-permute-done.28 = f32[4,2,48,256]{3,2,1,0:T(8,128)S(1)} collective-permute-done((f32[4,2,48,256]{3,2,1,0:T(8,128)S(1)}, f32[4,2,48,256]{3,2,1,0:T(8,128)S(1)}, u32[]{:S(2)}, u32[]{:S(2)}) %collective-permute-start.28) | collective-permute-done | bytes 393248 | tf_op jit(solution)/shard_map/ppermute | solution.py:41
  104.5 0.1 add.120
  104.6 2.1 %collective-permute-start.30 = (f32[2,48,256]{2,1,0:T(8,128)S(1)}, f32[2,48,256]{2,1,0:T(8,128)S(1)}, u32[]{:S(2)}, u32[]{:S(2)}) collective-permute-start(f32[2,48,256]{2,1,0:T(8,128)S(1)} %get-tuple-element.16), channel_id=1, source_target_pairs={{0,4},{1,5},{2,6},{3,7},{4,0},{5,1},{6,2},{7,3},{8,12},{9,13},{10,... | collective-permute-start | bytes 294920 | tf_op jit(solution)/shard_map/ppermute | solution.py:41
  106.7 1.0 collective-permute-start.31
  107.7 2.4 %collective-permute-done.30 = f32[2,48,256]{2,1,0:T(8,128)S(1)} collective-permute-done((f32[2,48,256]{2,1,0:T(8,128)S(1)}, f32[2,48,256]{2,1,0:T(8,128)S(1)}, u32[]{:S(2)}, u32[]{:S(2)}) %collective-permute-start.30) | collective-permute-done | bytes 98336 | tf_op jit(solution)/shard_map/ppermute | solution.py:41
  110.1 2.2 %collective-permute-done.31 = f32[2,48,256]{2,1,0:T(8,128)S(1)} collective-permute-done((f32[2,48,256]{2,1,0:T(8,128)S(1)}, f32[2,48,256]{2,1,0:T(8,128)S(1)}, u32[]{:S(2)}, u32[]{:S(2)}) %collective-permute-start.31) | collective-permute-done | bytes 98336 | tf_op jit(solution)/shard_map/ppermute | solution.py:41
  112.4 5.8 %collective-permute-start.32 = (f32[48,256]{1,0:T(8,128)S(1)}, f32[48,256]{1,0:T(8,128)S(1)}, u32[]{:S(2)}, u32[]{:S(2)}) collective-permute-start(f32[48,256]{1,0:T(8,128)S(1)} %slice_bitcast_fusion.4), channel_id=1, source_target_pairs={{0,8},{1,9},{2,10},{3,11},{4,12},{5,13},{6,14},{7,15},{8,0},{9,1},... | collective-permute-start | bytes 147464 | tf_op jit(solution)/shard_map/ppermute | solution.py:41
  118.2 1.5 %collective-permute-done.32 = f32[48,256]{1,0:T(8,128)S(1)} collective-permute-done((f32[48,256]{1,0:T(8,128)S(1)}, f32[48,256]{1,0:T(8,128)S(1)}, u32[]{:S(2)}, u32[]{:S(2)}) %collective-permute-start.32) | collective-permute-done | bytes 49184 | tf_op jit(solution)/shard_map/ppermute | solution.py:41
  119.7 0.6 fusion.1
  (44 shorter events, 0.3 us)
Async XLA Ops:
  7.5 11.9 %collective-permute-start.2 = (f32[4,48,256]{2,1,0:T(8,128)S(1)}, f32[4,48,256]{2,1,0:T(8,128)S(1)}, u32[]{:S(2)}, u32[]{:S(2)}) collective-permute-start(f32[4,48,256]{2,1,0:T(8,128)S(1)} %bitcast.65), channel_id=1, source_target_pairs={{0,192},{16,208},{32,224},{48,240},{64,128},{80,144},{96,160},{112... | collective-permute-start | bytes 589832 | tf_op jit(solution)/shard_map/ppermute | solution.py:31
  11.1 8.3 %collective-permute-start.1 = (f32[4,48,256]{2,1,0:T(8,128)S(1)}, f32[4,48,256]{2,1,0:T(8,128)S(1)}, u32[]{:S(2)}, u32[]{:S(2)}) collective-permute-start(f32[4,48,256]{2,1,0:T(8,128)S(1)} %bitcast.64), channel_id=1, source_target_pairs={{0,128},{16,144},{32,160},{48,176},{64,192},{80,208},{96,224},{112... | collective-permute-start | bytes 589832 | tf_op jit(solution)/shard_map/ppermute | solution.py:31
  11.5 8.0 %collective-permute-start = (f32[4,48,256]{2,1,0:T(8,128)S(1)}, f32[4,48,256]{2,1,0:T(8,128)S(1)}, u32[]{:S(2)}, u32[]{:S(2)}) collective-permute-start(f32[4,48,256]{2,1,0:T(8,128)S(1)} %bitcast.63), channel_id=1, source_target_pairs={{0,64},{16,80},{32,96},{48,112},{64,0},{80,16},{96,32},{112,48},{1... | collective-permute-start | bytes 589832 | tf_op jit(solution)/shard_map/ppermute | solution.py:31
  19.5 69.1 %copy-start = (f32[768,256]{1,0:T(8,128)S(1)}, f32[768,256]{1,0:T(8,128)}, u32[]{:S(2)}) copy-start(f32[768,256]{1,0:T(8,128)} %targets_ref.1) | copy-start | bytes 2359300
  19.5 8.4 %collective-permute-start.4 = (f32[48,256]{1,0:T(8,128)S(1)}, f32[48,256]{1,0:T(8,128)S(1)}, u32[]{:S(2)}, u32[]{:S(2)}) collective-permute-start(f32[48,256]{1,0:T(8,128)S(1)} %get-tuple-element.19), channel_id=1, source_target_pairs={{0,32},{16,48},{32,0},{48,16},{64,96},{80,112},{96,64},{112,80},{1... | collective-permute-start | bytes 147464 | tf_op jit(solution)/shard_map/ppermute | solution.py:31
  23.5 5.3 %collective-permute-start.5 = (f32[48,256]{1,0:T(8,128)S(1)}, f32[48,256]{1,0:T(8,128)S(1)}, u32[]{:S(2)}, u32[]{:S(2)}) collective-permute-start(f32[48,256]{1,0:T(8,128)S(1)} %get-tuple-element.20), channel_id=1, source_target_pairs={{0,48},{16,32},{32,16},{48,0},{64,112},{80,96},{96,80},{112,64},{1... | collective-permute-start | bytes 147464 | tf_op jit(solution)/shard_map/ppermute | solution.py:31
  24.9 3.8 %collective-permute-start.3 = (f32[48,256]{1,0:T(8,128)S(1)}, f32[48,256]{1,0:T(8,128)S(1)}, u32[]{:S(2)}, u32[]{:S(2)}) collective-permute-start(f32[48,256]{1,0:T(8,128)S(1)} %get-tuple-element.21), channel_id=1, source_target_pairs={{0,16},{16,0},{32,48},{48,32},{64,80},{80,64},{96,112},{112,96},{1... | collective-permute-start | bytes 147464 | tf_op jit(solution)/shard_map/ppermute | solution.py:31
  25.1 9.3 %collective-permute-start.20 = (f32[64,256]{1,0:T(8,128)S(1)}, f32[64,256]{1,0:T(8,128)S(1)}, u32[]{:S(2)}, u32[]{:S(2)}) collective-permute-start(f32[64,256]{1,0:T(8,128)S(1)} %slice.84), channel_id=1, source_target_pairs={{0,192},{16,208},{32,224},{48,240},{64,128},{80,144},{96,160},{112... | collective-permute-start | bytes 196616 | tf_op jit(solution)/shard_map/ppermute | solution.py:31
  27.8 6.6 %collective-permute-start.19 = (f32[64,256]{1,0:T(8,128)S(1)}, f32[64,256]{1,0:T(8,128)S(1)}, u32[]{:S(2)}, u32[]{:S(2)}) collective-permute-start(f32[64,256]{1,0:T(8,128)S(1)} %slice.84), channel_id=1, source_target_pairs={{0,128},{16,144},{32,160},{48,176},{64,192},{80,208},{96,224},{112... | collective-permute-start | bytes 196616 | tf_op jit(solution)/shard_map/ppermute | solution.py:31
  27.9 6.5 %collective-permute-start.18 = (f32[64,256]{1,0:T(8,128)S(1)}, f32[64,256]{1,0:T(8,128)S(1)}, u32[]{:S(2)}, u32[]{:S(2)}) collective-permute-start(f32[64,256]{1,0:T(8,128)S(1)} %slice.84), channel_id=1, source_target_pairs={{0,64},{16,80},{32,96},{48,112},{64,0},{80,16},{96,32},{112,48},{1... | collective-permute-start | bytes 196616 | tf_op jit(solution)/shard_map/ppermute | solution.py:31
  28.8 15.3 %collective-permute-start.6 = (f32[48,256]{1,0:T(8,128)S(1)}, f32[48,256]{1,0:T(8,128)S(1)}, u32[]{:S(2)}, u32[]{:S(2)}) collective-permute-start(f32[48,256]{1,0:T(8,128)S(1)} %fusion.2), channel_id=1, source_target_pairs={{0,8},{1,9},{2,10},{3,11},{4,12},{5,13},{6,14},{7,15},{8,0},{9,1},... | collective-permute-start | bytes 147464 | tf_op jit(solution)/shard_map/ppermute | solution.py:41
  34.4 13.3 %collective-permute-start.23 = (f32[64,256]{1,0:T(8,128)S(1)}, f32[64,256]{1,0:T(8,128)S(1)}, u32[]{:S(2)}, u32[]{:S(2)}) collective-permute-start(f32[64,256]{1,0:T(8,128)S(1)} %add_add_fusion.2), channel_id=1, source_target_pairs={{0,48},{16,32},{32,16},{48,0},{64,112},{80,96},{96,80},{112,64},{1... | collective-permute-start | bytes 196616 | tf_op jit(solution)/shard_map/ppermute | solution.py:31
  36.1 13.1 %collective-permute-start.22 = (f32[64,256]{1,0:T(8,128)S(1)}, f32[64,256]{1,0:T(8,128)S(1)}, u32[]{:S(2)}, u32[]{:S(2)}) collective-permute-start(f32[64,256]{1,0:T(8,128)S(1)} %add_add_fusion.2), channel_id=1, source_target_pairs={{0,32},{16,48},{32,0},{48,16},{64,96},{80,112},{96,64},{112,80},{1... | collective-permute-start | bytes 196616 | tf_op jit(solution)/shard_map/ppermute | solution.py:31
  36.5 12.8 %collective-permute-start.21 = (f32[64,256]{1,0:T(8,128)S(1)}, f32[64,256]{1,0:T(8,128)S(1)}, u32[]{:S(2)}, u32[]{:S(2)}) collective-permute-start(f32[64,256]{1,0:T(8,128)S(1)} %add_add_fusion.2), channel_id=1, source_target_pairs={{0,16},{16,0},{32,48},{48,32},{64,80},{80,64},{96,112},{112,96},{1... | collective-permute-start | bytes 196616 | tf_op jit(solution)/shard_map/ppermute | solution.py:31
  38.1 14.0 %collective-permute-start.11 = (f32[48,256]{1,0:T(8,128)S(1)}, f32[48,256]{1,0:T(8,128)S(1)}, u32[]{:S(2)}, u32[]{:S(2)}) collective-permute-start(f32[48,256]{1,0:T(8,128)S(1)} %fusion.2), channel_id=1, source_target_pairs={{0,0},{1,16},{2,32},{3,48},{4,64},{5,80},{6,96},{7,112},{8,128},{9... | collective-permute-start | bytes 147464 | tf_op jit(solution)/shard_map/ppermute | solution.py:46
  44.1 8.0 %collective-permute-start.8 = (f32[2,48,256]{2,1,0:T(8,128)S(1)}, f32[2,48,256]{2,1,0:T(8,128)S(1)}, u32[]{:S(2)}, u32[]{:S(2)}) collective-permute-start(f32[2,48,256]{2,1,0:T(8,128)S(1)} %get-tuple-element.23), channel_id=1, source_target_pairs={{0,4},{1,5},{2,6},{3,7},{4,0},{5,1},{6,2},{7,3},{8,12},{9,13},{10,... | collective-permute-start | bytes 294920 | tf_op jit(solution)/shard_map/ppermute | solution.py:41
  47.7 7.0 %collective-permute-start.7 = (f32[2,48,256]{2,1,0:T(8,128)S(1)}, f32[2,48,256]{2,1,0:T(8,128)S(1)}, u32[]{:S(2)}, u32[]{:S(2)}) collective-permute-start(f32[2,48,256]{2,1,0:T(8,128)S(1)} %get-tuple-element.23), channel_id=1, source_target_pairs={{0,2},{1,3},{2,0},{3,1},{4,6},{5,7},{6,4},{7,5},{8,10},{9,11},{10,... | collective-permute-start | bytes 294920 | tf_op jit(solution)/shard_map/ppermute | solution.py:41
  49.2 5.4 %collective-permute-start.9 = (f32[2,48,256]{2,1,0:T(8,128)S(1)}, f32[2,48,256]{2,1,0:T(8,128)S(1)}, u32[]{:S(2)}, u32[]{:S(2)}) collective-permute-start(f32[2,48,256]{2,1,0:T(8,128)S(1)} %get-tuple-element.23), channel_id=1, source_target_pairs={{0,6},{1,7},{2,4},{3,5},{4,2},{5,3},{6,0},{7,1},{8,14},{9,15},{10,... | collective-permute-start | bytes 294920 | tf_op jit(solution)/shard_map/ppermute | solution.py:41
  49.3 8.0 %collective-permute-start.26 = (f32[64,256]{1,0:T(8,128)S(1)}, f32[64,256]{1,0:T(8,128)S(1)}, u32[]{:S(2)}, u32[]{:S(2)}) collective-permute-start(f32[64,256]{1,0:T(8,128)S(1)} %add_add_fusion.1), channel_id=1, source_target_pairs={{0,6},{1,7},{2,4},{3,5},{4,2},{5,3},{6,0},{7,1},{8,14},{9,15},{10,... | collective-permute-start | bytes 196616 | tf_op jit(solution)/shard_map/ppermute | solution.py:41
  52.0 6.3 %collective-permute-start.25 = (f32[64,256]{1,0:T(8,128)S(1)}, f32[64,256]{1,0:T(8,128)S(1)}, u32[]{:S(2)}, u32[]{:S(2)}) collective-permute-start(f32[64,256]{1,0:T(8,128)S(1)} %add_add_fusion.1), channel_id=1, source_target_pairs={{0,4},{1,5},{2,6},{3,7},{4,0},{5,1},{6,2},{7,3},{8,12},{9,13},{10,... | collective-permute-start | bytes 196616 | tf_op jit(solution)/shard_map/ppermute | solution.py:41
  52.0 8.6 %collective-permute-start.24 = (f32[64,256]{1,0:T(8,128)S(1)}, f32[64,256]{1,0:T(8,128)S(1)}, u32[]{:S(2)}, u32[]{:S(2)}) collective-permute-start(f32[64,256]{1,0:T(8,128)S(1)} %add_add_fusion.1), channel_id=1, source_target_pairs={{0,2},{1,3},{2,0},{3,1},{4,6},{5,7},{6,4},{7,5},{8,10},{9,11},{10,... | collective-permute-start | bytes 196616 | tf_op jit(solution)/shard_map/ppermute | solution.py:41
  54.7 6.1 %collective-permute-start.14 = (f32[48,256]{1,0:T(8,128)S(1)}, f32[48,256]{1,0:T(8,128)S(1)}, u32[]{:S(2)}, u32[]{:S(2)}) collective-permute-start(f32[48,256]{1,0:T(8,128)S(1)} %collective-permute-done.11), channel_id=1, source_target_pairs={{0,48},{16,32},{32,16},{48,0},{64,112},{80,96},{96,80},{112,64},{1... | collective-permute-start | bytes 147464 | tf_op jit(solution)/shard_map/ppermute | solution.py:31
  54.7 6.1 %collective-permute-start.13 = (f32[48,256]{1,0:T(8,128)S(1)}, f32[48,256]{1,0:T(8,128)S(1)}, u32[]{:S(2)}, u32[]{:S(2)}) collective-permute-start(f32[48,256]{1,0:T(8,128)S(1)} %collective-permute-done.11), channel_id=1, source_target_pairs={{0,32},{16,48},{32,0},{48,16},{64,96},{80,112},{96,64},{112,80},{1... | collective-permute-start | bytes 147464 | tf_op jit(solution)/shard_map/ppermute | solution.py:31
  57.3 3.5 %collective-permute-start.12 = (f32[48,256]{1,0:T(8,128)S(1)}, f32[48,256]{1,0:T(8,128)S(1)}, u32[]{:S(2)}, u32[]{:S(2)}) collective-permute-start(f32[48,256]{1,0:T(8,128)S(1)} %collective-permute-done.11), channel_id=1, source_target_pairs={{0,16},{16,0},{32,48},{48,32},{64,80},{80,64},{96,112},{112,96},{1... | collective-permute-start | bytes 147464 | tf_op jit(solution)/shard_map/ppermute | solution.py:31
  58.3 30.3 %collective-permute-start.10 = (f32[4,2,48,256]{3,2,1,0:T(8,128)S(1)}, f32[4,2,48,256]{3,2,1,0:T(8,128)S(1)}, u32[]{:S(2)}, u32[]{:S(2)}) collective-permute-start(f32[4,2,48,256]{3,2,1,0:T(8,128)S(1)} %pad_maximum_fusion.own_rows), channel_id=1, source_target_pairs={{0,1},{1,0},{2,3},{3,2},{4,5},{5,4},{6,7},{7,6},{8,9},{9,8},{10,11... | collective-permute-start | bytes 1179656 | tf_op jit(solution)/shard_map/ppermute | solution.py:41
  60.6 6.0 %collective-permute-start.27 = (f32[4,64,256]{2,1,0:T(8,128)S(1)}, f32[4,64,256]{2,1,0:T(8,128)S(1)}, u32[]{:S(2)}, u32[]{:S(2)}) collective-permute-start(f32[4,64,256]{2,1,0:T(8,128)S(1)} %pad_maximum_fusion.1.own_ref), channel_id=1, source_target_pairs={{0,1},{1,0},{2,3},{3,2},{4,5},{5,4},{6,7},{7,6},{8,9},{9,8},{10,11... | collective-permute-start | bytes 786440 | tf_op jit(solution)/shard_map/ppermute | solution.py:41
  60.8 27.8 %collective-permute-start.17 = (f32[4,48,256]{2,1,0:T(8,128)S(1)}, f32[4,48,256]{2,1,0:T(8,128)S(1)}, u32[]{:S(2)}, u32[]{:S(2)}) collective-permute-start(f32[4,48,256]{2,1,0:T(8,128)S(1)} %pad_maximum_fusion.2.c0), channel_id=1, source_target_pairs={{0,192},{16,208},{32,224},{48,240},{64,128},{80,144},{96,160},{112... | collective-permute-start | bytes 589832 | tf_op jit(solution)/shard_map/ppermute | solution.py:31
  65.9 22.7 %collective-permute-start.16 = (f32[4,48,256]{2,1,0:T(8,128)S(1)}, f32[4,48,256]{2,1,0:T(8,128)S(1)}, u32[]{:S(2)}, u32[]{:S(2)}) collective-permute-start(f32[4,48,256]{2,1,0:T(8,128)S(1)} %pad_maximum_fusion.2.c0), channel_id=1, source_target_pairs={{0,128},{16,144},{32,160},{48,176},{64,192},{80,208},{96,224},{112... | collective-permute-start | bytes 589832 | tf_op jit(solution)/shard_map/ppermute | solution.py:31
  66.4 22.2 %collective-permute-start.15 = (f32[4,48,256]{2,1,0:T(8,128)S(1)}, f32[4,48,256]{2,1,0:T(8,128)S(1)}, u32[]{:S(2)}, u32[]{:S(2)}) collective-permute-start(f32[4,48,256]{2,1,0:T(8,128)S(1)} %pad_maximum_fusion.2.c0), channel_id=1, source_target_pairs={{0,64},{16,80},{32,96},{48,112},{64,0},{80,16},{96,32},{112,48},{1... | collective-permute-start | bytes 589832 | tf_op jit(solution)/shard_map/ppermute | solution.py:31
  100.3 4.2 %collective-permute-start.28 = (f32[4,2,48,256]{3,2,1,0:T(8,128)S(1)}, f32[4,2,48,256]{3,2,1,0:T(8,128)S(1)}, u32[]{:S(2)}, u32[]{:S(2)}) collective-permute-start(f32[4,2,48,256]{3,2,1,0:T(8,128)S(1)} %get-tuple-element.11), channel_id=1, source_target_pairs={{0,1},{1,0},{2,3},{3,2},{4,5},{5,4},{6,7},{7,6},{8,9},{9,8},{10,11... | collective-permute-start | bytes 1179656 | tf_op jit(solution)/shard_map/ppermute | solution.py:41
  104.6 5.6 %collective-permute-start.30 = (f32[2,48,256]{2,1,0:T(8,128)S(1)}, f32[2,48,256]{2,1,0:T(8,128)S(1)}, u32[]{:S(2)}, u32[]{:S(2)}) collective-permute-start(f32[2,48,256]{2,1,0:T(8,128)S(1)} %get-tuple-element.16), channel_id=1, source_target_pairs={{0,4},{1,5},{2,6},{3,7},{4,0},{5,1},{6,2},{7,3},{8,12},{9,13},{10,... | collective-permute-start | bytes 294920 | tf_op jit(solution)/shard_map/ppermute | solution.py:41
  106.7 5.6 %collective-permute-start.31 = (f32[2,48,256]{2,1,0:T(8,128)S(1)}, f32[2,48,256]{2,1,0:T(8,128)S(1)}, u32[]{:S(2)}, u32[]{:S(2)}) collective-permute-start(f32[2,48,256]{2,1,0:T(8,128)S(1)} %get-tuple-element.17), channel_id=1, source_target_pairs={{0,6},{1,7},{2,4},{3,5},{4,2},{5,3},{6,0},{7,1},{8,14},{9,15},{10,... | collective-permute-start | bytes 294920 | tf_op jit(solution)/shard_map/ppermute | solution.py:41
  107.7 4.6 %collective-permute-start.29 = (f32[2,48,256]{2,1,0:T(8,128)S(1)}, f32[2,48,256]{2,1,0:T(8,128)S(1)}, u32[]{:S(2)}, u32[]{:S(2)}) collective-permute-start(f32[2,48,256]{2,1,0:T(8,128)S(1)} %get-tuple-element.18), channel_id=1, source_target_pairs={{0,2},{1,3},{2,0},{3,1},{4,6},{5,7},{6,4},{7,5},{8,10},{9,11},{10,... | collective-permute-start | bytes 294920 | tf_op jit(solution)/shard_map/ppermute | solution.py:41
  112.4 7.3 %collective-permute-start.32 = (f32[48,256]{1,0:T(8,128)S(1)}, f32[48,256]{1,0:T(8,128)S(1)}, u32[]{:S(2)}, u32[]{:S(2)}) collective-permute-start(f32[48,256]{1,0:T(8,128)S(1)} %slice_bitcast_fusion.4), channel_id=1, source_target_pairs={{0,8},{1,9},{2,10},{3,11},{4,12},{5,13},{6,14},{7,15},{8,0},{9,1},... | collective-permute-start | bytes 147464 | tf_op jit(solution)/shard_map/ppermute | solution.py:41

commit v2 on v1

--- a/solution.py
+++ b/solution.py
@@ -187,7 +187,7 @@
     goal_high[...], goal_low[...] = split(targets_ref[...])
     lead_high[...], lead_low[...] = split(lead_ref[...] * -2.0)
     inv_high[...], inv_low[...] = split(inverse_ref[...])
-    cols, goal, inv, lead = (cols_high, cols_low), (goal_high, goal_low), (inv_high, inv_low), (lead_high, lead_low)
+    cols, goal, lead = (cols_high, cols_low), (goal_high, goal_low), (lead_high, lead_low)
     lead_lane = lane_squares(lead_ref[...])
     col_lane = lane_squares(cols_ref[...])
 
@@ -196,7 +196,14 @@
     gram = dot3(split(block), whole(goal), 1, 0)
     nuggets = [targets_ref[:NB, :] * jnp.where(col_place == p, nugget, 0.0) for p in range(PANELS)]
     gram = gram + jnp.concatenate(nuggets, axis=0)
-    weights = split(dot3(whole(inv), split(gram), 1, 0))
+    upper = (inv_high[:NB, :NB], inv_low[:NB, :NB])
+    lower = (inv_high[NB:, :], inv_low[NB:, :])
+    gram_high, gram_low = split(gram)
+    weights = split(
+        jnp.concatenate(
+            [dot3(upper, (gram_high[:NB], gram_low[:NB]), 1, 0), dot3(lower, (gram_high, gram_low), 1, 0)], axis=0
+        )
+    )
     same = jnp.where(row_place == col_place, nugget, 0.0)
 
     def starts_of(core):
@@ -211,7 +218,14 @@
         spot = jnp.where(row < NB, row + row_place * NB, LEAD)
         lane = lax.broadcasted_iota(jnp.int32, (HALF, LEAD), 1)
         block = block + jnp.where(spot == lane, nugget, 0.0)
-        panel = dot3(split(block), whole(inv), 1, 1)
+        high, low = split(block)
+        panel = jnp.concatenate(
+            [
+                dot3((high[:, :NB], low[:, :NB]), (inv_high[:NB, :NB], inv_low[:NB, :NB]), 1, 1),
+                dot3((high, low), (inv_high[NB:, :], inv_low[NB:, :]), 1, 1),
+            ],
+            axis=1,
+        )
         for n, start in enumerate(starts):
             panel_ref[pl.ds(start, PIECE), :] = panel[n * PIECE : n * PIECE + PIECE]
         return carry

time: 122 us -> 122 us (level)
  no operation moved by 1% of the time
where the time goes in v2:
time: 122 us; the launch traced here: 120 us
  starting transfers between devices  60.4 us (50%)
  Pallas kernels  33.3 us (27%)
  waiting for transfers between devices  17.6 us (14%)
  local copies, waits for them, and re-layouts  6.3 us (5%)
  other arithmetic  1.4 us (1%)
    pallas_call x4, Pallas kernels, call(): pl.pallas_call(kernel, out_shape=tuple((s if far else pltpu.VMEM(s.shape,...  33.3 us
    ppermute x14, starting transfers between devices, col_swap(): return lax.ppermute(value, 'col', pairs)  28.6 us
    ppermute x18, starting transfers between devices, row_swap(): return lax.ppermute(value, 'row', pairs)  25.8 us
    ppermute x14, waiting for transfers between devices, col_swap(): return lax.ppermute(value, 'col', pairs)  9.67 us
    ppermute x18, waiting for transfers between devices, row_swap(): return lax.ppermute(value, 'row', pairs)  7.91 us
    ppermute x1, starting transfers between devices, flip(): return lax.ppermute(value, ('row', 'col'), pairs)  5.97 us
    gather x1, local copies, waits for them, and re-layouts, per_device(): picked = jnp.take(archive, jnp.clip(ids, 0, shard - 1), axis=0)  4.87 us
  transfers between devices with their start and end apart: 33, of which 8 were waited for; matrix products, arithmetic and copies ran while one was open for 0% of the time, Pallas kernels for 18%

profile of v2, /device:TPU:1, one launch (start us, length us, event | category | flops | bytes accessed | tf_op | source)
XLA Modules:
  0.0 120.1 jit_solution(1346896466570177829)
XLA Ops:
  0.7 0.8 reshape.92
  1.6 0.1 dynamic-slice_bitcast_fusion
  1.7 0.1 dynamic_slice.6
  1.7 0.1 constant_dynamic-slice_fusion
  1.9 0.1 concatenate.26
  2.0 0.1 concatenate.23
  2.1 0.1 fusion.3
  2.2 0.1 compare_and_fusion.1
  2.3 4.9 %gather_fusion = f32[832,256]{1,0:T(8,128)S(1)} fusion(f32[4096,256]{1,0:T(8,128)} %param.3, s32[1024]{0:T(1024)S(1)} %pad_clamp_fusion), kind=kCustom, calls=%fused_computation | custom fusion | bytes 1707264 | tf_op jit(solution)/shard_map/jit(_take)/gather | solution.py:287
  7.1 0.3 select_select_fusion
  7.4 0.1 fusion.6
  7.5 3.6 %collective-permute-start.2 = (f32[4,48,256]{2,1,0:T(8,128)S(1)}, f32[4,48,256]{2,1,0:T(8,128)S(1)}, u32[]{:S(2)}, u32[]{:S(2)}) collective-permute-start(f32[4,48,256]{2,1,0:T(8,128)S(1)} %bitcast.65), channel_id=1, source_target_pairs={{0,192},{16,208},{32,224},{48,240},{64,128},{80,144},{96,160},{112... | collective-permute-start | bytes 589832 | tf_op jit(solution)/shard_map/ppermute | solution.py:31
  11.1 0.3 collective-permute-start.1
  11.5 0.3 collective-permute-start
  11.8 7.6 %collective-permute-done.2 = f32[4,48,256]{2,1,0:T(8,128)S(1)} collective-permute-done((f32[4,48,256]{2,1,0:T(8,128)S(1)}, f32[4,48,256]{2,1,0:T(8,128)S(1)}, u32[]{:S(2)}, u32[]{:S(2)}) %collective-permute-start.2) | collective-permute-done | bytes 196640 | tf_op jit(solution)/shard_map/ppermute | solution.py:31
  19.4 0.0 collective-permute-done.1
  19.4 0.0 collective-permute-done
  19.4 0.1 add_add_fusion
  19.5 0.0 copy-start
  19.5 3.9 %collective-permute-start.4 = (f32[48,256]{1,0:T(8,128)S(1)}, f32[48,256]{1,0:T(8,128)S(1)}, u32[]{:S(2)}, u32[]{:S(2)}) collective-permute-start(f32[48,256]{1,0:T(8,128)S(1)} %get-tuple-element.19), channel_id=1, source_target_pairs={{0,32},{16,48},{32,0},{48,16},{64,96},{80,112},{96,64},{112,80},{1... | collective-permute-start | bytes 147464 | tf_op jit(solution)/shard_map/ppermute | solution.py:31
  23.5 1.5 %collective-permute-start.5 = (f32[48,256]{1,0:T(8,128)S(1)}, f32[48,256]{1,0:T(8,128)S(1)}, u32[]{:S(2)}, u32[]{:S(2)}) collective-permute-start(f32[48,256]{1,0:T(8,128)S(1)} %get-tuple-element.20), channel_id=1, source_target_pairs={{0,48},{16,32},{32,16},{48,0},{64,112},{80,96},{96,80},{112,64},{1... | collective-permute-start | bytes 147464 | tf_op jit(solution)/shard_map/ppermute | solution.py:31
  24.9 0.2 collective-permute-start.3
  25.1 2.7 %collective-permute-start.20 = (f32[64,256]{1,0:T(8,128)S(1)}, f32[64,256]{1,0:T(8,128)S(1)}, u32[]{:S(2)}, u32[]{:S(2)}) collective-permute-start(f32[64,256]{1,0:T(8,128)S(1)} %slice.84), channel_id=1, source_target_pairs={{0,192},{16,208},{32,224},{48,240},{64,128},{80,144},{96,160},{112... | collective-permute-start | bytes 196616 | tf_op jit(solution)/shard_map/ppermute | solution.py:31
  27.8 0.1 collective-permute-start.19
  27.9 0.0 collective-permute-done.4
  27.9 0.6 collective-permute-start.18
  28.5 0.2 collective-permute-done.5
  28.8 5.6 %collective-permute-start.6 = (f32[48,256]{1,0:T(8,128)S(1)}, f32[48,256]{1,0:T(8,128)S(1)}, u32[]{:S(2)}, u32[]{:S(2)}) collective-permute-start(f32[48,256]{1,0:T(8,128)S(1)} %fusion.2), channel_id=1, source_target_pairs={{0,8},{1,9},{2,10},{3,11},{4,12},{5,13},{6,14},{7,15},{8,0},{9,1},... | collective-permute-start | bytes 147464 | tf_op jit(solution)/shard_map/ppermute | solution.py:41
  34.4 0.0 collective-permute-done.20
  34.4 0.0 collective-permute-done.19
  34.4 0.0 collective-permute-done.18
  34.4 1.7 %collective-permute-start.23 = (f32[64,256]{1,0:T(8,128)S(1)}, f32[64,256]{1,0:T(8,128)S(1)}, u32[]{:S(2)}, u32[]{:S(2)}) collective-permute-start(f32[64,256]{1,0:T(8,128)S(1)} %add_add_fusion.2), channel_id=1, source_target_pairs={{0,48},{16,32},{32,16},{48,0},{64,112},{80,96},{96,80},{112,64},{1... | collective-permute-start | bytes 196616 | tf_op jit(solution)/shard_map/ppermute | solution.py:31
  36.1 0.3 collective-permute-start.22
  36.5 1.6 %collective-permute-start.21 = (f32[64,256]{1,0:T(8,128)S(1)}, f32[64,256]{1,0:T(8,128)S(1)}, u32[]{:S(2)}, u32[]{:S(2)}) collective-permute-start(f32[64,256]{1,0:T(8,128)S(1)} %add_add_fusion.2), channel_id=1, source_target_pairs={{0,16},{16,0},{32,48},{48,32},{64,80},{80,64},{96,112},{112,96},{1... | collective-permute-start | bytes 196616 | tf_op jit(solution)/shard_map/ppermute | solution.py:31
  38.1 6.0 %collective-permute-start.11 = (f32[48,256]{1,0:T(8,128)S(1)}, f32[48,256]{1,0:T(8,128)S(1)}, u32[]{:S(2)}, u32[]{:S(2)}) collective-permute-start(f32[48,256]{1,0:T(8,128)S(1)} %fusion.2), channel_id=1, source_target_pairs={{0,0},{1,16},{2,32},{3,48},{4,64},{5,80},{6,96},{7,112},{8,128},{9... | collective-permute-start | bytes 147464 | tf_op jit(solution)/shard_map/ppermute | solution.py:46
  44.1 3.6 %collective-permute-start.8 = (f32[2,48,256]{2,1,0:T(8,128)S(1)}, f32[2,48,256]{2,1,0:T(8,128)S(1)}, u32[]{:S(2)}, u32[]{:S(2)}) collective-permute-start(f32[2,48,256]{2,1,0:T(8,128)S(1)} %get-tuple-element.23), channel_id=1, source_target_pairs={{0,4},{1,5},{2,6},{3,7},{4,0},{5,1},{6,2},{7,3},{8,12},{9,13},{10,... | collective-permute-start | bytes 294920 | tf_op jit(solution)/shard_map/ppermute | solution.py:41
  47.7 1.5 %collective-permute-start.7 = (f32[2,48,256]{2,1,0:T(8,128)S(1)}, f32[2,48,256]{2,1,0:T(8,128)S(1)}, u32[]{:S(2)}, u32[]{:S(2)}) collective-permute-start(f32[2,48,256]{2,1,0:T(8,128)S(1)} %get-tuple-element.23), channel_id=1, source_target_pairs={{0,2},{1,3},{2,0},{3,1},{4,6},{5,7},{6,4},{7,5},{8,10},{9,11},{10,... | collective-permute-start | bytes 294920 | tf_op jit(solution)/shard_map/ppermute | solution.py:41
  49.3 2.8 %collective-permute-start.26 = (f32[64,256]{1,0:T(8,128)S(1)}, f32[64,256]{1,0:T(8,128)S(1)}, u32[]{:S(2)}, u32[]{:S(2)}) collective-permute-start(f32[64,256]{1,0:T(8,128)S(1)} %add_add_fusion.1), channel_id=1, source_target_pairs={{0,6},{1,7},{2,4},{3,5},{4,2},{5,3},{6,0},{7,1},{8,14},{9,15},{10,... | collective-permute-start | bytes 196616 | tf_op jit(solution)/shard_map/ppermute | solution.py:41
  52.0 1.0 collective-permute-start.24
  53.0 1.6 %collective-permute-done.7 = f32[2,48,256]{2,1,0:T(8,128)S(1)} collective-permute-done((f32[2,48,256]{2,1,0:T(8,128)S(1)}, f32[2,48,256]{2,1,0:T(8,128)S(1)}, u32[]{:S(2)}, u32[]{:S(2)}) %collective-permute-start.7) | collective-permute-done | bytes 98336 | tf_op jit(solution)/shard_map/ppermute | solution.py:41
  54.7 0.0 collective-permute-start.14
  54.7 2.0 %collective-permute-start.13 = (f32[48,256]{1,0:T(8,128)S(1)}, f32[48,256]{1,0:T(8,128)S(1)}, u32[]{:S(2)}, u32[]{:S(2)}) collective-permute-start(f32[48,256]{1,0:T(8,128)S(1)} %collective-permute-done.11), channel_id=1, source_target_pairs={{0,32},{16,48},{32,0},{48,16},{64,96},{80,112},{96,64},{112,80},{1... | collective-permute-start | bytes 147464 | tf_op jit(solution)/shard_map/ppermute | solution.py:31
  56.7 0.6 collective-permute-done.26
  57.3 1.1 collective-permute-start.12
  58.3 2.3 %collective-permute-start.10 = (f32[4,2,48,256]{3,2,1,0:T(8,128)S(1)}, f32[4,2,48,256]{3,2,1,0:T(8,128)S(1)}, u32[]{:S(2)}, u32[]{:S(2)}) collective-permute-start(f32[4,2,48,256]{3,2,1,0:T(8,128)S(1)} %pad_maximum_fusion.own_rows), channel_id=1, source_target_pairs={{0,1},{1,0},{2,3},{3,2},{4,5},{5,4},{6,7},{7,6},{8,9},{9,8},{10,11... | collective-permute-start | bytes 1179656 | tf_op jit(solution)/shard_map/ppermute | solution.py:41
  60.6 0.1 collective-permute-start.27
  60.8 5.1 %collective-permute-start.17 = (f32[4,48,256]{2,1,0:T(8,128)S(1)}, f32[4,48,256]{2,1,0:T(8,128)S(1)}, u32[]{:S(2)}, u32[]{:S(2)}) collective-permute-start(f32[4,48,256]{2,1,0:T(8,128)S(1)} %pad_maximum_fusion.2.c0), channel_id=1, source_target_pairs={{0,192},{16,208},{32,224},{48,240},{64,128},{80,144},{96,160},{112... | collective-permute-start | bytes 589832 | tf_op jit(solution)/shard_map/ppermute | solution.py:31
  65.9 0.5 collective-permute-start.16
  66.4 0.2 collective-permute-start.15
  66.6 0.1 stack.85.place_ref
  66.7 1.8 %shard_map.50 = (f32[512,256]{1,0:T(8,128)S(1)}, f32[512,512]{1,0:T(8,128)S(1)}) custom-call(s32[7]{0:T(128)S(1)} %stack.85.place_ref, f32[4,64,256]{2,1,0:T(8,128)S(1)} %pad_maximum_fusion.1.own_ref, f32[4,64,256]{2,1,0:T(8,128)S(1)} %collective-permute-done.27.other_ref), custom_call_target="tpu_custom_call" | custom-call | tf_op jit(solution)/shard_map/pallas_call | solution.py:263
  68.4 10.4 %shard_map.51.in_ref = f32[512,512]{1,0:T(8,128)S(1)} custom-call(f32[512,512]{1,0:T(8,128)S(1)} %get-tuple-element.8.in_ref), custom_call_target="tpu_custom_call" | custom-call | tf_op jit(solution)/shard_map/pallas_call | solution.py:263
  78.8 9.8 %shard_map.52.inverse_ref = f32[512,512]{1,0:T(8,128)S(1)} custom-call(f32[512,512]{1,0:T(8,128)S(1)} %shard_map.51.in_ref), custom_call_target="tpu_custom_call" | custom-call | tf_op jit(solution)/shard_map/pallas_call | solution.py:263
  88.6 11.4 %shard_map.53 = (f32[768,512]{1,0:T(8,128)}, f32[4,2,48,256]{3,2,1,0:T(8,128)S(1)}, f32[4,2,48,256]{3,2,1,0:T(8,128)S(1)}) custom-call(s32[7]{0:T(128)S(1)} %stack.85.place_ref, f32[4,2,48,256]{3,2,1,0:T(8,128)S(1)} %pad_maximum_fusion.own_rows, f32[4,2,48,256]{3,2,1,0:T(8,128)S(1)} %collective-permute-done.10.other_rows, ...), custom_call_target="tpu_custom_call" | custom-call | tf_op jit(solution)/shard_map/pallas_call | solution.py:263
  100.1 2.8 %collective-permute-start.28 = (f32[4,2,48,256]{3,2,1,0:T(8,128)S(1)}, f32[4,2,48,256]{3,2,1,0:T(8,128)S(1)}, u32[]{:S(2)}, u32[]{:S(2)}) collective-permute-start(f32[4,2,48,256]{3,2,1,0:T(8,128)S(1)} %get-tuple-element.11), channel_id=1, source_target_pairs={{0,1},{1,0},{2,3},{3,2},{4,5},{5,4},{6,7},{7,6},{8,9},{9,8},{10,11... | collective-permute-start | bytes 1179656 | tf_op jit(solution)/shard_map/ppermute | solution.py:41
  102.9 1.3 %collective-permute-done.28 = f32[4,2,48,256]{3,2,1,0:T(8,128)S(1)} collective-permute-done((f32[4,2,48,256]{3,2,1,0:T(8,128)S(1)}, f32[4,2,48,256]{3,2,1,0:T(8,128)S(1)}, u32[]{:S(2)}, u32[]{:S(2)}) %collective-permute-start.28) | collective-permute-done | bytes 393248 | tf_op jit(solution)/shard_map/ppermute | solution.py:41
  104.3 0.1 add.120
  104.3 2.1 %collective-permute-start.30 = (f32[2,48,256]{2,1,0:T(8,128)S(1)}, f32[2,48,256]{2,1,0:T(8,128)S(1)}, u32[]{:S(2)}, u32[]{:S(2)}) collective-permute-start(f32[2,48,256]{2,1,0:T(8,128)S(1)} %get-tuple-element.16), channel_id=1, source_target_pairs={{0,4},{1,5},{2,6},{3,7},{4,0},{5,1},{6,2},{7,3},{8,12},{9,13},{10,... | collective-permute-start | bytes 294920 | tf_op jit(solution)/shard_map/ppermute | solution.py:41
  106.5 1.0 collective-permute-start.31
  107.5 2.4 %collective-permute-done.30 = f32[2,48,256]{2,1,0:T(8,128)S(1)} collective-permute-done((f32[2,48,256]{2,1,0:T(8,128)S(1)}, f32[2,48,256]{2,1,0:T(8,128)S(1)}, u32[]{:S(2)}, u32[]{:S(2)}) %collective-permute-start.30) | collective-permute-done | bytes 98336 | tf_op jit(solution)/shard_map/ppermute | solution.py:41
  109.9 2.2 %collective-permute-done.31 = f32[2,48,256]{2,1,0:T(8,128)S(1)} collective-permute-done((f32[2,48,256]{2,1,0:T(8,128)S(1)}, f32[2,48,256]{2,1,0:T(8,128)S(1)}, u32[]{:S(2)}, u32[]{:S(2)}) %collective-permute-start.31) | collective-permute-done | bytes 98336 | tf_op jit(solution)/shard_map/ppermute | solution.py:41
  112.1 5.8 %collective-permute-start.32 = (f32[48,256]{1,0:T(8,128)S(1)}, f32[48,256]{1,0:T(8,128)S(1)}, u32[]{:S(2)}, u32[]{:S(2)}) collective-permute-start(f32[48,256]{1,0:T(8,128)S(1)} %slice_bitcast_fusion.4), channel_id=1, source_target_pairs={{0,8},{1,9},{2,10},{3,11},{4,12},{5,13},{6,14},{7,15},{8,0},{9,1},... | collective-permute-start | bytes 147464 | tf_op jit(solution)/shard_map/ppermute | solution.py:41
  117.9 1.5 %collective-permute-done.32 = f32[48,256]{1,0:T(8,128)S(1)} collective-permute-done((f32[48,256]{1,0:T(8,128)S(1)}, f32[48,256]{1,0:T(8,128)S(1)}, u32[]{:S(2)}, u32[]{:S(2)}) %collective-permute-start.32) | collective-permute-done | bytes 49184 | tf_op jit(solution)/shard_map/ppermute | solution.py:41
  119.4 0.6 fusion.1
  (44 shorter events, 0.3 us)
Async XLA Ops:
  7.5 11.9 %collective-permute-start.2 = (f32[4,48,256]{2,1,0:T(8,128)S(1)}, f32[4,48,256]{2,1,0:T(8,128)S(1)}, u32[]{:S(2)}, u32[]{:S(2)}) collective-permute-start(f32[4,48,256]{2,1,0:T(8,128)S(1)} %bitcast.65), channel_id=1, source_target_pairs={{0,192},{16,208},{32,224},{48,240},{64,128},{80,144},{96,160},{112... | collective-permute-start | bytes 589832 | tf_op jit(solution)/shard_map/ppermute | solution.py:31
  11.1 8.3 %collective-permute-start.1 = (f32[4,48,256]{2,1,0:T(8,128)S(1)}, f32[4,48,256]{2,1,0:T(8,128)S(1)}, u32[]{:S(2)}, u32[]{:S(2)}) collective-permute-start(f32[4,48,256]{2,1,0:T(8,128)S(1)} %bitcast.64), channel_id=1, source_target_pairs={{0,128},{16,144},{32,160},{48,176},{64,192},{80,208},{96,224},{112... | collective-permute-start | bytes 589832 | tf_op jit(solution)/shard_map/ppermute | solution.py:31
  11.5 8.0 %collective-permute-start = (f32[4,48,256]{2,1,0:T(8,128)S(1)}, f32[4,48,256]{2,1,0:T(8,128)S(1)}, u32[]{:S(2)}, u32[]{:S(2)}) collective-permute-start(f32[4,48,256]{2,1,0:T(8,128)S(1)} %bitcast.63), channel_id=1, source_target_pairs={{0,64},{16,80},{32,96},{48,112},{64,0},{80,16},{96,32},{112,48},{1... | collective-permute-start | bytes 589832 | tf_op jit(solution)/shard_map/ppermute | solution.py:31
  19.5 69.1 %copy-start = (f32[768,256]{1,0:T(8,128)S(1)}, f32[768,256]{1,0:T(8,128)}, u32[]{:S(2)}) copy-start(f32[768,256]{1,0:T(8,128)} %targets_ref.1) | copy-start | bytes 2359300
  19.5 8.4 %collective-permute-start.4 = (f32[48,256]{1,0:T(8,128)S(1)}, f32[48,256]{1,0:T(8,128)S(1)}, u32[]{:S(2)}, u32[]{:S(2)}) collective-permute-start(f32[48,256]{1,0:T(8,128)S(1)} %get-tuple-element.19), channel_id=1, source_target_pairs={{0,32},{16,48},{32,0},{48,16},{64,96},{80,112},{96,64},{112,80},{1... | collective-permute-start | bytes 147464 | tf_op jit(solution)/shard_map/ppermute | solution.py:31
  23.5 5.3 %collective-permute-start.5 = (f32[48,256]{1,0:T(8,128)S(1)}, f32[48,256]{1,0:T(8,128)S(1)}, u32[]{:S(2)}, u32[]{:S(2)}) collective-permute-start(f32[48,256]{1,0:T(8,128)S(1)} %get-tuple-element.20), channel_id=1, source_target_pairs={{0,48},{16,32},{32,16},{48,0},{64,112},{80,96},{96,80},{112,64},{1... | collective-permute-start | bytes 147464 | tf_op jit(solution)/shard_map/ppermute | solution.py:31
  24.9 3.8 %collective-permute-start.3 = (f32[48,256]{1,0:T(8,128)S(1)}, f32[48,256]{1,0:T(8,128)S(1)}, u32[]{:S(2)}, u32[]{:S(2)}) collective-permute-start(f32[48,256]{1,0:T(8,128)S(1)} %get-tuple-element.21), channel_id=1, source_target_pairs={{0,16},{16,0},{32,48},{48,32},{64,80},{80,64},{96,112},{112,96},{1... | collective-permute-start | bytes 147464 | tf_op jit(solution)/shard_map/ppermute | solution.py:31
  25.1 9.3 %collective-permute-start.20 = (f32[64,256]{1,0:T(8,128)S(1)}, f32[64,256]{1,0:T(8,128)S(1)}, u32[]{:S(2)}, u32[]{:S(2)}) collective-permute-start(f32[64,256]{1,0:T(8,128)S(1)} %slice.84), channel_id=1, source_target_pairs={{0,192},{16,208},{32,224},{48,240},{64,128},{80,144},{96,160},{112... | collective-permute-start | bytes 196616 | tf_op jit(solution)/shard_map/ppermute | solution.py:31
  27.8 6.6 %collective-permute-start.19 = (f32[64,256]{1,0:T(8,128)S(1)}, f32[64,256]{1,0:T(8,128)S(1)}, u32[]{:S(2)}, u32[]{:S(2)}) collective-permute-start(f32[64,256]{1,0:T(8,128)S(1)} %slice.84), channel_id=1, source_target_pairs={{0,128},{16,144},{32,160},{48,176},{64,192},{80,208},{96,224},{112... | collective-permute-start | bytes 196616 | tf_op jit(solution)/shard_map/ppermute | solution.py:31
  27.9 6.5 %collective-permute-start.18 = (f32[64,256]{1,0:T(8,128)S(1)}, f32[64,256]{1,0:T(8,128)S(1)}, u32[]{:S(2)}, u32[]{:S(2)}) collective-permute-start(f32[64,256]{1,0:T(8,128)S(1)} %slice.84), channel_id=1, source_target_pairs={{0,64},{16,80},{32,96},{48,112},{64,0},{80,16},{96,32},{112,48},{1... | collective-permute-start | bytes 196616 | tf_op jit(solution)/shard_map/ppermute | solution.py:31
  28.8 15.3 %collective-permute-start.6 = (f32[48,256]{1,0:T(8,128)S(1)}, f32[48,256]{1,0:T(8,128)S(1)}, u32[]{:S(2)}, u32[]{:S(2)}) collective-permute-start(f32[48,256]{1,0:T(8,128)S(1)} %fusion.2), channel_id=1, source_target_pairs={{0,8},{1,9},{2,10},{3,11},{4,12},{5,13},{6,14},{7,15},{8,0},{9,1},... | collective-permute-start | bytes 147464 | tf_op jit(solution)/shard_map/ppermute | solution.py:41
  34.4 13.3 %collective-permute-start.23 = (f32[64,256]{1,0:T(8,128)S(1)}, f32[64,256]{1,0:T(8,128)S(1)}, u32[]{:S(2)}, u32[]{:S(2)}) collective-permute-start(f32[64,256]{1,0:T(8,128)S(1)} %add_add_fusion.2), channel_id=1, source_target_pairs={{0,48},{16,32},{32,16},{48,0},{64,112},{80,96},{96,80},{112,64},{1... | collective-permute-start | bytes 196616 | tf_op jit(solution)/shard_map/ppermute | solution.py:31
  36.1 13.1 %collective-permute-start.22 = (f32[64,256]{1,0:T(8,128)S(1)}, f32[64,256]{1,0:T(8,128)S(1)}, u32[]{:S(2)}, u32[]{:S(2)}) collective-permute-start(f32[64,256]{1,0:T(8,128)S(1)} %add_add_fusion.2), channel_id=1, source_target_pairs={{0,32},{16,48},{32,0},{48,16},{64,96},{80,112},{96,64},{112,80},{1... | collective-permute-start | bytes 196616 | tf_op jit(solution)/shard_map/ppermute | solution.py:31
  36.5 12.8 %collective-permute-start.21 = (f32[64,256]{1,0:T(8,128)S(1)}, f32[64,256]{1,0:T(8,128)S(1)}, u32[]{:S(2)}, u32[]{:S(2)}) collective-permute-start(f32[64,256]{1,0:T(8,128)S(1)} %add_add_fusion.2), channel_id=1, source_target_pairs={{0,16},{16,0},{32,48},{48,32},{64,80},{80,64},{96,112},{112,96},{1... | collective-permute-start | bytes 196616 | tf_op jit(solution)/shard_map/ppermute | solution.py:31
  38.1 14.0 %collective-permute-start.11 = (f32[48,256]{1,0:T(8,128)S(1)}, f32[48,256]{1,0:T(8,128)S(1)}, u32[]{:S(2)}, u32[]{:S(2)}) collective-permute-start(f32[48,256]{1,0:T(8,128)S(1)} %fusion.2), channel_id=1, source_target_pairs={{0,0},{1,16},{2,32},{3,48},{4,64},{5,80},{6,96},{7,112},{8,128},{9... | collective-permute-start | bytes 147464 | tf_op jit(solution)/shard_map/ppermute | solution.py:46
  44.1 8.0 %collective-permute-start.8 = (f32[2,48,256]{2,1,0:T(8,128)S(1)}, f32[2,48,256]{2,1,0:T(8,128)S(1)}, u32[]{:S(2)}, u32[]{:S(2)}) collective-permute-start(f32[2,48,256]{2,1,0:T(8,128)S(1)} %get-tuple-element.23), channel_id=1, source_target_pairs={{0,4},{1,5},{2,6},{3,7},{4,0},{5,1},{6,2},{7,3},{8,12},{9,13},{10,... | collective-permute-start | bytes 294920 | tf_op jit(solution)/shard_map/ppermute | solution.py:41
  47.7 7.0 %collective-permute-start.7 = (f32[2,48,256]{2,1,0:T(8,128)S(1)}, f32[2,48,256]{2,1,0:T(8,128)S(1)}, u32[]{:S(2)}, u32[]{:S(2)}) collective-permute-start(f32[2,48,256]{2,1,0:T(8,128)S(1)} %get-tuple-element.23), channel_id=1, source_target_pairs={{0,2},{1,3},{2,0},{3,1},{4,6},{5,7},{6,4},{7,5},{8,10},{9,11},{10,... | collective-permute-start | bytes 294920 | tf_op jit(solution)/shard_map/ppermute | solution.py:41
  49.2 5.4 %collective-permute-start.9 = (f32[2,48,256]{2,1,0:T(8,128)S(1)}, f32[2,48,256]{2,1,0:T(8,128)S(1)}, u32[]{:S(2)}, u32[]{:S(2)}) collective-permute-start(f32[2,48,256]{2,1,0:T(8,128)S(1)} %get-tuple-element.23), channel_id=1, source_target_pairs={{0,6},{1,7},{2,4},{3,5},{4,2},{5,3},{6,0},{7,1},{8,14},{9,15},{10,... | collective-permute-start | bytes 294920 | tf_op jit(solution)/shard_map/ppermute | solution.py:41
  49.3 8.0 %collective-permute-start.26 = (f32[64,256]{1,0:T(8,128)S(1)}, f32[64,256]{1,0:T(8,128)S(1)}, u32[]{:S(2)}, u32[]{:S(2)}) collective-permute-start(f32[64,256]{1,0:T(8,128)S(1)} %add_add_fusion.1), channel_id=1, source_target_pairs={{0,6},{1,7},{2,4},{3,5},{4,2},{5,3},{6,0},{7,1},{8,14},{9,15},{10,... | collective-permute-start | bytes 196616 | tf_op jit(solution)/shard_map/ppermute | solution.py:41
  52.0 6.3 %collective-permute-start.25 = (f32[64,256]{1,0:T(8,128)S(1)}, f32[64,256]{1,0:T(8,128)S(1)}, u32[]{:S(2)}, u32[]{:S(2)}) collective-permute-start(f32[64,256]{1,0:T(8,128)S(1)} %add_add_fusion.1), channel_id=1, source_target_pairs={{0,4},{1,5},{2,6},{3,7},{4,0},{5,1},{6,2},{7,3},{8,12},{9,13},{10,... | collective-permute-start | bytes 196616 | tf_op jit(solution)/shard_map/ppermute | solution.py:41
  52.0 8.6 %collective-permute-start.24 = (f32[64,256]{1,0:T(8,128)S(1)}, f32[64,256]{1,0:T(8,128)S(1)}, u32[]{:S(2)}, u32[]{:S(2)}) collective-permute-start(f32[64,256]{1,0:T(8,128)S(1)} %add_add_fusion.1), channel_id=1, source_target_pairs={{0,2},{1,3},{2,0},{3,1},{4,6},{5,7},{6,4},{7,5},{8,10},{9,11},{10,... | collective-permute-start | bytes 196616 | tf_op jit(solution)/shard_map/ppermute | solution.py:41
  54.7 6.1 %collective-permute-start.14 = (f32[48,256]{1,0:T(8,128)S(1)}, f32[48,256]{1,0:T(8,128)S(1)}, u32[]{:S(2)}, u32[]{:S(2)}) collective-permute-start(f32[48,256]{1,0:T(8,128)S(1)} %collective-permute-done.11), channel_id=1, source_target_pairs={{0,48},{16,32},{32,16},{48,0},{64,112},{80,96},{96,80},{112,64},{1... | collective-permute-start | bytes 147464 | tf_op jit(solution)/shard_map/ppermute | solution.py:31
  54.7 6.1 %collective-permute-start.13 = (f32[48,256]{1,0:T(8,128)S(1)}, f32[48,256]{1,0:T(8,128)S(1)}, u32[]{:S(2)}, u32[]{:S(2)}) collective-permute-start(f32[48,256]{1,0:T(8,128)S(1)} %collective-permute-done.11), channel_id=1, source_target_pairs={{0,32},{16,48},{32,0},{48,16},{64,96},{80,112},{96,64},{112,80},{1... | collective-permute-start | bytes 147464 | tf_op jit(solution)/shard_map/ppermute | solution.py:31
  57.3 3.5 %collective-permute-start.12 = (f32[48,256]{1,0:T(8,128)S(1)}, f32[48,256]{1,0:T(8,128)S(1)}, u32[]{:S(2)}, u32[]{:S(2)}) collective-permute-start(f32[48,256]{1,0:T(8,128)S(1)} %collective-permute-done.11), channel_id=1, source_target_pairs={{0,16},{16,0},{32,48},{48,32},{64,80},{80,64},{96,112},{112,96},{1... | collective-permute-start | bytes 147464 | tf_op jit(solution)/shard_map/ppermute | solution.py:31
  58.3 30.3 %collective-permute-start.10 = (f32[4,2,48,256]{3,2,1,0:T(8,128)S(1)}, f32[4,2,48,256]{3,2,1,0:T(8,128)S(1)}, u32[]{:S(2)}, u32[]{:S(2)}) collective-permute-start(f32[4,2,48,256]{3,2,1,0:T(8,128)S(1)} %pad_maximum_fusion.own_rows), channel_id=1, source_target_pairs={{0,1},{1,0},{2,3},{3,2},{4,5},{5,4},{6,7},{7,6},{8,9},{9,8},{10,11... | collective-permute-start | bytes 1179656 | tf_op jit(solution)/shard_map/ppermute | solution.py:41
  60.6 6.0 %collective-permute-start.27 = (f32[4,64,256]{2,1,0:T(8,128)S(1)}, f32[4,64,256]{2,1,0:T(8,128)S(1)}, u32[]{:S(2)}, u32[]{:S(2)}) collective-permute-start(f32[4,64,256]{2,1,0:T(8,128)S(1)} %pad_maximum_fusion.1.own_ref), channel_id=1, source_target_pairs={{0,1},{1,0},{2,3},{3,2},{4,5},{5,4},{6,7},{7,6},{8,9},{9,8},{10,11... | collective-permute-start | bytes 786440 | tf_op jit(solution)/shard_map/ppermute | solution.py:41
  60.8 27.8 %collective-permute-start.17 = (f32[4,48,256]{2,1,0:T(8,128)S(1)}, f32[4,48,256]{2,1,0:T(8,128)S(1)}, u32[]{:S(2)}, u32[]{:S(2)}) collective-permute-start(f32[4,48,256]{2,1,0:T(8,128)S(1)} %pad_maximum_fusion.2.c0), channel_id=1, source_target_pairs={{0,192},{16,208},{32,224},{48,240},{64,128},{80,144},{96,160},{112... | collective-permute-start | bytes 589832 | tf_op jit(solution)/shard_map/ppermute | solution.py:31
  65.9 22.7 %collective-permute-start.16 = (f32[4,48,256]{2,1,0:T(8,128)S(1)}, f32[4,48,256]{2,1,0:T(8,128)S(1)}, u32[]{:S(2)}, u32[]{:S(2)}) collective-permute-start(f32[4,48,256]{2,1,0:T(8,128)S(1)} %pad_maximum_fusion.2.c0), channel_id=1, source_target_pairs={{0,128},{16,144},{32,160},{48,176},{64,192},{80,208},{96,224},{112... | collective-permute-start | bytes 589832 | tf_op jit(solution)/shard_map/ppermute | solution.py:31
  66.4 22.2 %collective-permute-start.15 = (f32[4,48,256]{2,1,0:T(8,128)S(1)}, f32[4,48,256]{2,1,0:T(8,128)S(1)}, u32[]{:S(2)}, u32[]{:S(2)}) collective-permute-start(f32[4,48,256]{2,1,0:T(8,128)S(1)} %pad_maximum_fusion.2.c0), channel_id=1, source_target_pairs={{0,64},{16,80},{32,96},{48,112},{64,0},{80,16},{96,32},{112,48},{1... | collective-permute-start | bytes 589832 | tf_op jit(solution)/shard_map/ppermute | solution.py:31
  100.1 4.2 %collective-permute-start.28 = (f32[4,2,48,256]{3,2,1,0:T(8,128)S(1)}, f32[4,2,48,256]{3,2,1,0:T(8,128)S(1)}, u32[]{:S(2)}, u32[]{:S(2)}) collective-permute-start(f32[4,2,48,256]{3,2,1,0:T(8,128)S(1)} %get-tuple-element.11), channel_id=1, source_target_pairs={{0,1},{1,0},{2,3},{3,2},{4,5},{5,4},{6,7},{7,6},{8,9},{9,8},{10,11... | collective-permute-start | bytes 1179656 | tf_op jit(solution)/shard_map/ppermute | solution.py:41
  104.3 5.6 %collective-permute-start.30 = (f32[2,48,256]{2,1,0:T(8,128)S(1)}, f32[2,48,256]{2,1,0:T(8,128)S(1)}, u32[]{:S(2)}, u32[]{:S(2)}) collective-permute-start(f32[2,48,256]{2,1,0:T(8,128)S(1)} %get-tuple-element.16), channel_id=1, source_target_pairs={{0,4},{1,5},{2,6},{3,7},{4,0},{5,1},{6,2},{7,3},{8,12},{9,13},{10,... | collective-permute-start | bytes 294920 | tf_op jit(solution)/shard_map/ppermute | solution.py:41
  106.5 5.6 %collective-permute-start.31 = (f32[2,48,256]{2,1,0:T(8,128)S(1)}, f32[2,48,256]{2,1,0:T(8,128)S(1)}, u32[]{:S(2)}, u32[]{:S(2)}) collective-permute-start(f32[2,48,256]{2,1,0:T(8,128)S(1)} %get-tuple-element.17), channel_id=1, source_target_pairs={{0,6},{1,7},{2,4},{3,5},{4,2},{5,3},{6,0},{7,1},{8,14},{9,15},{10,... | collective-permute-start | bytes 294920 | tf_op jit(solution)/shard_map/ppermute | solution.py:41
  107.5 4.6 %collective-permute-start.29 = (f32[2,48,256]{2,1,0:T(8,128)S(1)}, f32[2,48,256]{2,1,0:T(8,128)S(1)}, u32[]{:S(2)}, u32[]{:S(2)}) collective-permute-start(f32[2,48,256]{2,1,0:T(8,128)S(1)} %get-tuple-element.18), channel_id=1, source_target_pairs={{0,2},{1,3},{2,0},{3,1},{4,6},{5,7},{6,4},{7,5},{8,10},{9,11},{10,... | collective-permute-start | bytes 294920 | tf_op jit(solution)/shard_map/ppermute | solution.py:41
  112.1 7.3 %collective-permute-start.32 = (f32[48,256]{1,0:T(8,128)S(1)}, f32[48,256]{1,0:T(8,128)S(1)}, u32[]{:S(2)}, u32[]{:S(2)}) collective-permute-start(f32[48,256]{1,0:T(8,128)S(1)} %slice_bitcast_fusion.4), channel_id=1, source_target_pairs={{0,8},{1,9},{2,10},{3,11},{4,12},{5,13},{6,14},{7,15},{8,0},{9,1},... | collective-permute-start | bytes 147464 | tf_op jit(solution)/shard_map/ppermute | solution.py:41
